TPU v7x, 512 devices: a whole 4x8x8 slice. The times are simulated.
512 devices in a mesh: ops: 128 (over x, z_hi, y), grp: 4 (over z_lo, core).
Axes of the slice: x: 4, y: 8, z: 8 (z_hi: 4, z_lo: 2; z = z_hi * 2 + z_lo), core: 2. Of those that a mesh axis runs over, the one named last changes fastest.
Arguments:
- wave: bfloat16 [32, 512, 512], P(None, 'ops'), may hold values from -12 to 12
- diag_energy: float32 [32, 512, 512], P(None, 'ops'), may hold values from 0.5 to 2
- left_ops: bfloat16 [512, 512, 512], P(('ops', 'grp')), may hold values from -0.046875 to 0.046875
- right_ops: bfloat16 [512, 512, 512], P(('ops', 'grp')), may hold values from -0.25 to 0.25
- pair_sectors: int32 [512, 2], replicated, may hold values from 0 to 31, all different within a row
- sector_slot: int32 [32], replicated, may hold values from 0 to 31, each once
Outputs:
- residual: float32 [32, 512, 512], P(None, 'ops', 'grp')
- sigma_out: float32 [32, 512, 512], P(None, 'ops', 'grp')
Inputs may be any that keep to these rules, and one draw needn't show every extreme that they name: `pair_sectors`: each row names two different sectors; every sector is named by some row. `sector_slot`: each slot once.
All inputs are finite; a program needn't handle non-finite values.
Results may differ from a plain program's by a relative error of at most 0.0062.
Values may be sent and summed in bfloat16 or wider, within the bound.
No kernel may reach another device: no remote copies, remote signals or barrier semaphores. Data moves between devices by JAX's collectives and lax.ppermute only.
A program may use at most 64 MiB of HBM per device.

v0:
```python
import jax
import jax.numpy as jnp
from jax import lax
from jax.sharding import Mesh
from jax.sharding import PartitionSpec as P

OPS = ("ops_0", "ops_1", "ops_2")
OPS_GRP = ("ops_0", "ops_1", "ops_2", "grp")


def from_everyone(value, axis):
    devices = lax.axis_size(axis)
    return lax.all_to_all(
        jnp.broadcast_to(value[None], (devices, *value.shape)), axis, 0, 0, tiled=True
    )


def taken_together(value, axis):
    everything = from_everyone(value, axis)
    return jnp.sum(everything, axis=0)


def over_axes(value, axes):
    for axis in axes:
        value = lax.psum(value, axis)
    return value


def segment_total(received, targets, sectors):
    choose = (targets[None, :] == jnp.arange(sectors, dtype=jnp.int32)[:, None]).astype(jnp.float32)
    return jnp.dot(
        choose, received, precision=lax.Precision.HIGHEST, preferred_element_type=jnp.float32
    )


def apply_pairs(vector, left_ops, right_ops, wanted):
    ops_count = lax.axis_size(OPS)
    sectors, rows_here, block_width = vector.shape
    pair_dev = left_ops.shape[0]
    cell_count = rows_here * block_width
    outgoing = jnp.take(vector, wanted.reshape(-1), axis=0).reshape(
        ops_count, pair_dev * 2, rows_here, block_width
    )
    fetched = lax.all_to_all(outgoing, OPS, split_axis=0, concat_axis=2, tiled=True)
    inner_half = jnp.einsum(
        "pij,pjk->pik", left_ops, fetched[:, 0], preferred_element_type=jnp.float32
    ).astype(jnp.bfloat16)
    forward = jnp.einsum("pik,pkl->pil", inner_half, right_ops, preferred_element_type=jnp.float32)
    flipped = jnp.einsum(
        "pji,pjk->pik", left_ops, fetched[:, 1], preferred_element_type=jnp.float32
    ).astype(jnp.bfloat16)
    adjoint = jnp.einsum("pik,plk->pil", flipped, right_ops, preferred_element_type=jnp.float32)
    stacked = jnp.stack((adjoint, forward), axis=1).reshape(
        pair_dev, 2, ops_count, rows_here, block_width
    )
    arrived = lax.all_to_all(
        stacked.astype(jnp.bfloat16), OPS, split_axis=2, concat_axis=2, tiled=True
    ).astype(stacked.dtype)
    targets = jnp.transpose(wanted, (1, 2, 0)).reshape(-1)
    summed = segment_total(arrived.reshape(-1, cell_count), targets, sectors)
    return summed.reshape(sectors, rows_here, block_width)


def reduce_group(partial_value):
    return taken_together(partial_value, "grp")


def body(wave, diag_energy, left_ops, right_ops, pair_sectors, sector_slot):
    ops_count = lax.axis_size(OPS)
    grp_count = lax.axis_size("grp")
    pair_dev = left_ops.shape[0]
    block_width = wave.shape[2]
    stored = jnp.take(sector_slot, pair_sectors, axis=0).reshape(ops_count, grp_count, pair_dev, 2)
    wanted = lax.dynamic_index_in_dim(stored, lax.axis_index("grp"), 1, keepdims=False)
    column_share = block_width // grp_count
    column_start = lax.axis_index("grp") * column_share
    applied_sum = reduce_group(apply_pairs(wave, left_ops, right_ops, wanted))
    wave_wide = wave.astype(jnp.float32)
    applied = diag_energy * wave_wide + applied_sum
    products = (
        over_axes(jnp.sum(wave_wide * applied), OPS),
        over_axes(jnp.sum(wave_wide * wave_wide), OPS),
    )
    rayleigh = products[0] / products[1]
    residual = applied - rayleigh * wave_wide
    residual_half = residual.astype(jnp.bfloat16)
    second = reduce_group(apply_pairs(residual_half, left_ops, right_ops, wanted))
    sigma_out = diag_energy * residual_half.astype(jnp.float32) + second
    return (
        lax.dynamic_slice_in_dim(residual, column_start, column_share, 2),
        lax.dynamic_slice_in_dim(sigma_out, column_start, column_share, 2),
    )


def solution(mesh):
    finer = Mesh(
        mesh.devices.reshape(4, 4, 8, mesh.shape["grp"]), ("ops_0", "ops_1", "ops_2", "grp")
    )
    return jax.shard_map(
        body,
        mesh=finer,
        in_specs=(
            P(None, OPS, None),
            P(None, OPS, None),
            P(OPS_GRP, None, None),
            P(OPS_GRP, None, None),
            P(),
            P(),
        ),
        out_specs=(P(None, OPS, "grp"), P(None, OPS, "grp")),
        check_vma=False,
    )
```

profile of v0, /device:TPU:1, one launch (start us, length us, event | category | flops | bytes accessed | tf_op | source)
XLA Modules:
  0.0 287.8 jit_solution(8234370538445215668)
XLA Ops:
  0.7 0.7 copy-done.4
  1.4 0.7 fusion.45
  2.1 0.7 fusion.44
  3.5 20.1 %and_select_fusion = s32[512,2]{0,1:T(2,128)S(1)} fusion(s32[512,2]{0,1:T(2,128)S(1)} %copy-done.5, s32[]{:T(128)} %bitcast, s32[]{:T(128)} %bitcast.1, s32[]{:T(128)} %bitcast.2, s32[]{:T(128)} %bitcast.3, s32[]{:T(128)} %bitcast.4, s32[]{:T(128)} %bitcast.5, s32[]{:T(128)} %bitcast.6, s32[]{:T(128)} %bitcast.7, s32[]{:T(128)} %bitcast.8, s32[]{:T(128)} %bitcast.9, ...), kind=kLoop, calls=%fused_computation.90 | loop fusion | flops 70656 | bytes 8320 | tf_op jit(solution)/shard_map/jit(_take)/select_n | solution.py:73
  23.9 0.9 copy.73
  25.0 1.5 gather_fusion
  26.5 1.0 broadcast_select_fusion.1
  27.6 0.8 copy.74
  28.4 51.8 %all_to_all.56 = bf16[128,2,4,512]{3,1,2,0:T(2,128)(2,1)S(1)} all-to-all(bf16[128,2,4,512]{3,1,2,0:T(2,128)(2,1)S(1)} %copy.74), channel_id=1, replica_groups=mesh['ops_0'=4,'ops_1'=4,'ops_2'=8,'grp'=4] {'ops_0','ops_1','ops_2'}, dimensions={0} | all-to-all | bytes 2097152 | tf_op jit(solution)/shard_map/all_to_all | solution.py:44
  80.2 1.5 fusion.43
  83.0 0.9 copy-done.6
  84.9 0.8 copy.77
  85.7 37.7 %all_to_all.57 = bf16[1,2,128,4,512]{4,3,1,0,2:T(4,128)(2,1)S(1)} all-to-all(bf16[1,2,128,4,512]{4,3,1,0,2:T(4,128)(2,1)S(1)} %copy.77), channel_id=1, replica_groups=mesh['ops_0'=4,'ops_1'=4,'ops_2'=8,'grp'=4] {'ops_0','ops_1','ops_2'}, dimensions={2} | all-to-all | bytes 2097152 | tf_op jit(solution)/shard_map/all_to_all | solution.py:56
  125.1 19.2 %all_to_all.58 = f32[4,32,4,512]{3,1,2,0:T(8,128)S(1)} all-to-all(f32[4,32,4,512]{3,1,2,0:T(8,128)S(1)} %broadcast_in_dim.31), channel_id=1, replica_groups=mesh['ops_0'=4,'ops_1'=4,'ops_2'=8,'grp'=4] {'grp'}, dimensions={0} | all-to-all | bytes 2097152 | tf_op jit(solution)/shard_map/all_to_all | solution.py:13
  144.4 0.9 copy-done.2
  145.3 0.8 fusion.30
  146.1 7.0 %all-reduce.2 = (f32[]{:T(128)}, f32[]{:T(128)}) all-reduce(f32[]{:T(128)} %get-tuple-element.6, f32[]{:T(128)} %get-tuple-element.5), channel_id=1, replica_groups=mesh['ops_0'=4,'ops_1'=4,'ops_2'=8,'grp'=4] {'ops_0'}, use_global_device_ids=true, to_apply=%region_2.4 | all-reduce | flops 2 | bytes 16 | tf_op jit(solution)/shard_map/psum | solution.py:25
  153.1 9.5 %all-reduce.1 = (f32[]{:T(128)}, f32[]{:T(128)}) all-reduce(f32[]{:T(128)} %get-tuple-element.11, f32[]{:T(128)} %get-tuple-element.12), channel_id=1, replica_groups=mesh['ops_0'=4,'ops_1'=4,'ops_2'=8,'grp'=4] {'ops_1'}, use_global_device_ids=true, to_apply=%region_3.5 | all-reduce | flops 2 | bytes 16 | tf_op jit(solution)/shard_map/psum | solution.py:25
  162.6 11.6 %all-reduce = (f32[]{:T(128)}, f32[]{:T(128)}) all-reduce(f32[]{:T(128)} %get-tuple-element.9, f32[]{:T(128)} %get-tuple-element.10), channel_id=1, replica_groups=mesh['ops_0'=4,'ops_1'=4,'ops_2'=8,'grp'=4] {'ops_2'}, use_global_device_ids=true, to_apply=%region_4.6 | all-reduce | flops 2 | bytes 16 | tf_op jit(solution)/shard_map/psum | solution.py:25
  175.7 1.5 gather_fusion.1
  177.3 1.0 broadcast_select_fusion
  178.3 0.8 copy.81
  179.2 32.8 %all_to_all.59 = bf16[128,2,4,512]{3,1,2,0:T(2,128)(2,1)S(1)} all-to-all(bf16[128,2,4,512]{3,1,2,0:T(2,128)(2,1)S(1)} %copy.81), channel_id=1, replica_groups=mesh['ops_0'=4,'ops_1'=4,'ops_2'=8,'grp'=4] {'ops_0','ops_1','ops_2'}, dimensions={0} | all-to-all | bytes 2097152 | tf_op jit(solution)/shard_map/all_to_all | solution.py:44
  212.0 1.5 fusion.42
  213.5 1.3 fusion.3
  215.4 0.9 copy-done.7
  218.0 0.8 copy.84
  218.8 44.7 %all_to_all.60 = bf16[1,2,128,4,512]{4,3,1,0,2:T(4,128)(2,1)S(1)} all-to-all(bf16[1,2,128,4,512]{4,3,1,0,2:T(4,128)(2,1)S(1)} %copy.84), channel_id=1, replica_groups=mesh['ops_0'=4,'ops_1'=4,'ops_2'=8,'grp'=4] {'ops_0','ops_1','ops_2'}, dimensions={2} | all-to-all | bytes 2097152 | tf_op jit(solution)/shard_map/all_to_all | solution.py:56
  265.2 1.1 broadcast_in_dim.32
  266.3 7.2 %all-to-all-start.5 = ((f32[4,32,4,512]{3,1,2,0:T(8,128)}), f32[4,32,4,512]{3,1,2,0:T(8,128)S(1)}, u32[]{:S(2)}, u32[]{:S(2)}) async-start(f32[4,32,4,512]{3,1,2,0:T(8,128)} %broadcast_in_dim.32), calls=%async_computation.5 | async-start | bytes 2097152 | tf_op jit(solution)/shard_map/all_to_all | solution.py:13
  274.2 12.8 %all-to-all-done.5 = f32[4,32,4,512]{3,1,2,0:T(8,128)S(1)} async-done(((f32[4,32,4,512]{3,1,2,0:T(8,128)}), f32[4,32,4,512]{3,1,2,0:T(8,128)S(1)}, u32[]{:S(2)}, u32[]{:S(2)}) %all-to-all-start.5) | async-done | bytes 1048608 | tf_op jit(solution)/shard_map/all_to_all | solution.py:13
  287.1 0.7 copy_add_fusion
  (45 shorter events, 10.0 us)
Async XLA Ops:
  0.6 81.1 %copy-start = (bf16[1,512,512]{2,1,0:T(8,128)(2,1)S(1)}, bf16[1,512,512]{2,1,0:T(8,128)(2,1)}, u32[]{:S(2)}) copy-start(bf16[1,512,512]{2,1,0:T(8,128)(2,1)} %param.10) | copy-start | bytes 1572868
  0.6 0.7 copy-start.4
  2.8 0.7 copy-start.5
  23.9 1.1 copy-start.1
  82.8 1.0 copy-start.6
  144.3 1.0 copy-start.2
  215.2 1.0 copy-start.7
  216.3 1.0 copy-start.3
  266.3 20.7 %all-to-all-start.5 = ((f32[4,32,4,512]{3,1,2,0:T(8,128)}), f32[4,32,4,512]{3,1,2,0:T(8,128)S(1)}, u32[]{:S(2)}, u32[]{:S(2)}) async-start(f32[4,32,4,512]{3,1,2,0:T(8,128)} %broadcast_in_dim.32), calls=%async_computation.5 | async-start | bytes 2097152 | tf_op jit(solution)/shard_map/all_to_all | solution.py:13
where the time goes:
time: 289 us; the launch traced here: 288 us
  blocking collectives  214 us (74%)
  other arithmetic  24.4 us (8%)
  local copies, waits for them, and re-layouts  21.5 us (7%)
  waiting for transfers between devices  12.8 us (4%)
  starting transfers between devices  7.25 us (3%)
  matrix products  5.27 us (2%)
    all_to_all x2, blocking collectives, apply_pairs(): lax.all_to_all(outgoing, OPS, split_axis=0, concat_axis=2, tiled=True)  84.6 us
    all_to_all x2, blocking collectives, apply_pairs(): lax.all_to_all(stacked.astype(jnp.bfloat16), OPS, split_axis=2, concat_ax...  82.5 us
    psum x3, blocking collectives, over_axes(): value = lax.psum(value, axis)  28 us
    select_n x1, other arithmetic, body(): jnp.take(sector_slot, pair_sectors, axis=0)  20.1 us
    all_to_all x1, blocking collectives, from_everyone(): lax.all_to_all(jnp.broadcast_to(value[None], (devices, *value.shape)), ax...  19.2 us
    all_to_all x1, waiting for transfers between devices, from_everyone(): lax.all_to_all(jnp.broadcast_to(value[None], (devices, *value.shape)), ax...  12.8 us
    all_to_all x1, starting transfers between devices, from_everyone(): lax.all_to_all(jnp.broadcast_to(value[None], (devices, *value.shape)), ax...  7.25 us
  transfers between devices with their start and end apart: 1, of which 1 were waited for; matrix products, arithmetic and copies ran while one was open for 0% of the time, Pallas kernels for 0%

commit v1 on v0

v1 whole, which is shorter than its diff:
```python
import functools

import jax
import jax.numpy as jnp
from jax import lax
from jax.experimental import pallas as pl
from jax.experimental.pallas import tpu as pltpu
from jax.sharding import Mesh
from jax.sharding import PartitionSpec as P

OPS = ("ops_0", "ops_1", "ops_2")
OPS_GRP = ("ops_0", "ops_1", "ops_2", "grp")
F32 = jnp.float32
BF16 = jnp.bfloat16
VMEM = pl.BlockSpec(memory_space=pltpu.VMEM)
CONTRACT_ROWS = (((0,), (0,)), ((), ()))
CONTRACT_COLUMNS = (((1,), (1,)), ((), ()))


def iota(shape, dim):
    return lax.broadcasted_iota(jnp.int32, shape, dim)


def one_hot(mask):
    return jnp.where(mask, 1.0, 0.0).astype(BF16)


def whole(value):
    return value.astype(F32).astype(BF16)


def select_kernel(groups, ends_ref, slot_ref, wave_ref, choose_ref, out_ref):
    grp = lax.axis_index("grp")
    pairs = ends_ref.shape[1]
    ops = pairs // groups
    sectors = slot_ref.shape[1]
    rows_here = wave_ref.shape[0] // sectors
    mine = one_hot(iota((pairs, ops), 0) == iota((pairs, ops), 1) * groups + grp)
    sector = jnp.dot(whole(ends_ref[...]), mine, preferred_element_type=F32)
    slot_row = whole(slot_ref[...])
    number = iota((sectors, ops), 0).astype(F32)
    message = iota((ops, 2 * ops * rows_here), 1)
    holder = iota((ops, 2 * ops * rows_here), 0)
    target = jnp.zeros((1, 2 * ops * rows_here), F32)
    for end in range(2):
        slot = jnp.dot(slot_row, one_hot(number == sector[end : end + 1]), preferred_element_type=F32)
        spread = one_hot(message // rows_here == holder * 2 + end)
        target += jnp.dot(slot.astype(BF16), spread, preferred_element_type=F32)
    row = (iota(target.shape, 1) % rows_here).astype(F32)
    wanted = target * rows_here + row
    choose = one_hot(iota(choose_ref.shape, 0).astype(F32) == wanted)
    choose_ref[...] = choose
    out_ref[...] = lax.dot_general(
        choose, wave_ref[...], CONTRACT_ROWS, preferred_element_type=F32
    ).astype(BF16)


def pair_kernel(fetched_ref, left_ref, right_ref, out_ref):
    block = left_ref.shape[0]
    width = right_ref.shape[0]
    tiles = block // 8
    fetched = fetched_ref[...].astype(F32).reshape(tiles, 2, 8, width)
    first, second = fetched[:, 0], fetched[:, 1]
    upper = lax.broadcasted_iota(jnp.int32, first.shape, 1) < 4
    source = jnp.where(upper, first, pltpu.roll(second, 4, 1)).reshape(block, width).astype(BF16)
    target = jnp.where(upper, pltpu.roll(first, 4, 1), second).reshape(block, width).astype(BF16)
    left, right = left_ref[...], right_ref[...]
    inner = jnp.dot(left, source, preferred_element_type=F32).astype(BF16)
    forward = jnp.dot(inner, right, preferred_element_type=F32).reshape(tiles, 8, width)
    flipped = lax.dot_general(left, target, CONTRACT_ROWS, preferred_element_type=F32).astype(BF16)
    adjoint = lax.dot_general(
        flipped, right, CONTRACT_COLUMNS, preferred_element_type=F32
    ).reshape(tiles, 8, width)
    first = jnp.where(upper, adjoint, pltpu.roll(forward, 4, 1))
    second = jnp.where(upper, pltpu.roll(adjoint, 4, 1), forward)
    out_ref[...] = jnp.stack((first, second), axis=1).reshape(2 * block, width).astype(BF16)


def limit(mib):
    return pltpu.CompilerParams(vmem_limit_bytes=mib << 20)


def select_rows(ends, slots, wave_rows, groups):
    ops = ends.shape[1] // groups
    messages = 2 * ops * (wave_rows.shape[0] // slots.shape[1])
    return pl.pallas_call(
        functools.partial(select_kernel, groups),
        out_shape=(
            jax.ShapeDtypeStruct((wave_rows.shape[0], messages), BF16),
            jax.ShapeDtypeStruct((messages, wave_rows.shape[1]), BF16),
        ),
        in_specs=[VMEM] * 3,
        out_specs=(VMEM, VMEM),
        compiler_params=limit(24),
        cost_estimate=pl.CostEstimate(flops=400_000_000, bytes_accessed=2 << 20, transcendentals=0),
    )(ends, slots, wave_rows)


def apply_pair(fetched, left, right):
    return pl.pallas_call(
        pair_kernel,
        out_shape=jax.ShapeDtypeStruct(fetched.shape, BF16),
        in_specs=[VMEM] * 3,
        out_specs=VMEM,
        compiler_params=limit(24),
        cost_estimate=pl.CostEstimate(flops=1_100_000_000, bytes_accessed=3 << 20, transcendentals=0),
    )(fetched, left, right)


def exchange(rows, ops_count):
    shaped = rows.reshape(ops_count, rows.shape[0] // ops_count, rows.shape[1])
    return lax.all_to_all(shaped, OPS, 0, 0, tiled=True).reshape(rows.shape)


def taken_together(value, axes):
    devices = lax.axis_size(axes)
    copies = jnp.broadcast_to(value[None], (devices, *value.shape))
    return jnp.sum(lax.all_to_all(copies, axes, 0, 0, tiled=True), axis=0)


def body(wave, diag_energy, left_ops, right_ops, pair_sectors, sector_slot):
    ops_count = lax.axis_size(OPS)
    grp_count = lax.axis_size("grp")
    sectors, rows_here, width = wave.shape
    rows = sectors * rows_here
    share = width // grp_count
    left, right = left_ops[0], right_ops[0]
    wave_rows = wave.reshape(rows, width)
    diag_rows = diag_energy.reshape(rows, width)
    choose, outgoing = select_rows(pair_sectors.T, sector_slot[None], wave_rows, grp_count)

    def partial_blocks(outgoing):
        fetched = exchange(outgoing, ops_count)
        arrived = exchange(apply_pair(fetched, left, right), ops_count)
        return jnp.dot(choose, arrived, preferred_element_type=F32)

    summed = partial_blocks(outgoing)
    summed = summed + lax.ppermute(summed, "grp", [(g, g ^ 1) for g in range(grp_count)])
    summed = summed + lax.ppermute(
        summed.astype(BF16), "grp", [(g, g ^ 2) for g in range(grp_count)]
    ).astype(F32)
    wave_wide = wave_rows.astype(F32)
    applied = diag_rows * wave_wide + summed
    products = jnp.stack((jnp.sum(wave_wide * applied), jnp.sum(wave_wide * wave_wide)))
    products = taken_together(taken_together(products, "ops_2"), ("ops_0", "ops_1"))
    residual = applied - (products[0] / products[1]) * wave_wide
    residual_half = residual.astype(BF16)
    outgoing = lax.dot_general(
        choose, residual_half, CONTRACT_ROWS, preferred_element_type=F32
    ).astype(BF16)
    summed = partial_blocks(outgoing)
    parts = summed.astype(BF16).reshape(rows, grp_count, share).transpose(1, 0, 2)
    parts = lax.all_to_all(parts, "grp", 0, 0, tiled=True)
    start = lax.axis_index("grp") * share

    def mine(value):
        return lax.dynamic_slice_in_dim(value, start, share, 1)

    sigma_out = mine(diag_rows) * mine(residual_half).astype(F32) + jnp.sum(
        parts.astype(F32), axis=0
    )
    shape = (sectors, rows_here, share)
    return mine(residual).reshape(shape), sigma_out.reshape(shape)


def solution(mesh):
    finer = Mesh(
        mesh.devices.reshape(4, 4, 8, mesh.shape["grp"]), ("ops_0", "ops_1", "ops_2", "grp")
    )
    return jax.shard_map(
        body,
        mesh=finer,
        in_specs=(
            P(None, OPS, None),
            P(None, OPS, None),
            P(OPS_GRP, None, None),
            P(OPS_GRP, None, None),
            P(),
            P(),
        ),
        out_specs=(P(None, OPS, "grp"), P(None, OPS, "grp")),
        check_vma=False,
    )
```

time: 289 us -> 222 us (0.77)
  blocking collectives: 214 us -> 185 us
  other arithmetic: 24.4 us -> 3.64 us
  local copies, waits for them, and re-layouts: 21.5 us -> 4.29 us
  starting transfers between devices: 7.25 us -> 15.2 us
  waiting for transfers between devices: 12.8 us -> 6.97 us
  matrix products: 5.27 us -> 1.08 us
  Pallas kernels: 0 us -> 3.6 us
    psum x3 -> x0, blocking collectives: 28 us -> none  [over_axes(): value = lax.psum(value, axis)]
    select_n x4 -> x0, other arithmetic: 22.2 us -> none  [the longest x1 20.1 us: body(): jnp.take(sector_slot, pair_sectors, axis=0)]
    all_to_all x1, waiting for transfers between devices: 12.8 us -> 2.93 us  [body(): parts = lax.all_to_all(parts, 'grp', 0, 0, tiled=True)]
    ppermute x0 -> x2, starting transfers between devices: none -> 8.4 us  [the longest x1 5.59 us: body(): lax.ppermute(summed, 'grp', [(g, g ^ 1) for g in range(grp_count)])]
    gather x4 -> x0, local copies, waits for them, and re-layouts: 4.5 us -> none  [the longest x2 3.06 us: apply_pairs(): jnp.take(vector, wanted.reshape(-1), axis=0)]
    dot_general x10 -> x3, matrix products: 5.27 us -> 1.08 us  [the longest x2 0.63 us: partial_blocks(): return jnp.dot(choose, arrived, preferred_element_type=F32)]
    ppermute x0 -> x2, waiting for transfers between devices: none -> 4.04 us  [the longest x1 2.9 us: body(): lax.ppermute(summed.astype(BF16), 'grp', [(g, g ^ 2) for g in range(grp_c...]
    unnamed x18 -> x12, local copies, waits for them, and re-layouts: 5.2 us -> 1.36 us
  transfers between devices with their start and end apart: 1 -> 3, of which waited for: 1 -> 3; matrix products, arithmetic and copies ran while one was open for 0% -> 1% of each run, Pallas kernels for 0% -> 0%
where the time goes in v1:
time: 222 us
  blocking collectives  185 us (83%)
  starting transfers between devices  15.2 us (7%)
  waiting for transfers between devices  6.97 us (3%)
  local copies, waits for them, and re-layouts  4.29 us (2%)
  other arithmetic  3.64 us (2%)
  Pallas kernels  3.6 us (2%)
    all_to_all x4, blocking collectives, exchange(): return lax.all_to_all(shaped, OPS, 0, 0, tiled=True).reshape(rows.shape)  164 us
    all_to_all x2, blocking collectives, taken_together(): return jnp.sum(lax.all_to_all(copies, axes, 0, 0, tiled=True), axis=0)  21 us
    all_to_all x1, starting transfers between devices, body(): parts = lax.all_to_all(parts, 'grp', 0, 0, tiled=True)  6.77 us
    ppermute x1, starting transfers between devices, body(): lax.ppermute(summed, 'grp', [(g, g ^ 1) for g in range(grp_count)])  5.59 us
  transfers between devices with their start and end apart: 3, of which 3 were waited for; matrix products, arithmetic and copies ran while one was open for 1% of the time, Pallas kernels for 0%

profile of v1, /device:TPU:1, one launch (start us, length us, event | category | flops | bytes accessed | tf_op | source)
XLA Modules:
  0.0 221.8 jit_solution(5806041831259562350)
XLA Ops:
  0.6 0.9 reshape.57.wave_ref
  1.6 0.0 copy-start.2
  1.6 0.7 copy-done.2
  2.3 0.7 copy-done.3
  2.9 0.9 shard_map.77
  3.8 0.0 copy-start
  3.8 51.9 %all_to_all.37 = bf16[128,8,512]{2,1,0:T(8,128)(2,1)S(1)} all-to-all(bf16[128,8,512]{2,1,0:T(8,128)(2,1)S(1)} %bitcast.34), channel_id=1, replica_groups=mesh['ops_0'=4,'ops_1'=4,'ops_2'=8,'grp'=4] {'ops_0','ops_1','ops_2'}, dimensions={0} | all-to-all | bytes 2097152 | tf_op jit(solution)/shard_map/all_to_all | solution.py:112
  55.8 1.4 shard_map.78
  57.1 37.6 %all_to_all.38 = bf16[128,8,512]{2,1,0:T(8,128)(2,1)S(1)} all-to-all(bf16[128,8,512]{2,1,0:T(8,128)(2,1)S(1)} %bitcast.36), channel_id=1, replica_groups=mesh['ops_0'=4,'ops_1'=4,'ops_2'=8,'grp'=4] {'ops_0','ops_1','ops_2'}, dimensions={0} | all-to-all | bytes 2097152 | tf_op jit(solution)/shard_map/all_to_all | solution.py:112
  94.7 0.3 fusion.3
  95.0 5.6 %collective-permute-start = (f32[128,512]{1,0:T(8,128)S(1)}, f32[128,512]{1,0:T(8,128)S(1)}, u32[]{:S(2)}, u32[]{:S(2)}) collective-permute-start(f32[128,512]{1,0:T(8,128)S(1)} %fusion.3), channel_id=1, source_target_pairs={{0,1},{1,0},{2,3},{3,2},{4,5},{5,4},{6,7},{7,6},{8,9},{9,8},{10,11... | collective-permute-start | bytes 786440 | tf_op jit(solution)/shard_map/ppermute | solution.py:138
  100.6 1.1 collective-permute-done
  101.8 2.8 %collective-permute-start.1 = (bf16[128,512]{1,0:T(8,128)(2,1)S(1)}, bf16[128,512]{1,0:T(8,128)(2,1)S(1)}, u32[]{:S(2)}, u32[]{:S(2)}) collective-permute-start(bf16[128,512]{1,0:T(8,128)(2,1)S(1)} %get-tuple-element.8), channel_id=1, source_target_pairs={{0,2},{1,3},{2,0},{3,1},{4,6},{5,7},{6,4},{7,5},{8,10},{9,11},{10,... | collective-permute-start | bytes 393224 | tf_op jit(solution)/shard_map/ppermute | solution.py:139
  104.6 0.1 reshape.56
  104.7 0.7 multiply_reduce_fusion
  105.5 2.9 %collective-permute-done.1 = bf16[128,512]{1,0:T(8,128)(2,1)S(1)} collective-permute-done((bf16[128,512]{1,0:T(8,128)(2,1)S(1)}, bf16[128,512]{1,0:T(8,128)(2,1)S(1)}, u32[]{:S(2)}, u32[]{:S(2)}) %collective-permute-start.1) | collective-permute-done | bytes 131104 | tf_op jit(solution)/shard_map/ppermute | solution.py:139
  108.4 0.7 fusion.6
  109.1 1.4 pad_maximum_fusion
  110.4 8.9 %all_to_all.39 = f32[8,1,2]{2,1,0:T(1,128)S(1)} all-to-all(f32[8,1,2]{2,1,0:T(1,128)S(1)} %broadcast_in_dim.7), channel_id=1, replica_groups=mesh['ops_0'=4,'ops_1'=4,'ops_2'=8,'grp'=4] {'ops_2'}, dimensions={0} | all-to-all | bytes 128 | tf_op jit(solution)/shard_map/all_to_all | solution.py:118
  119.4 12.1 %all_to_all.40 = f32[16,1,2]{2,1,0:T(1,128)S(1)} all-to-all(f32[16,1,2]{2,1,0:T(1,128)S(1)} %broadcast_in_dim.8), channel_id=1, replica_groups=mesh['ops_0'=4,'ops_1'=4,'ops_2'=8,'grp'=4] {'ops_0','ops_1'}, dimensions={0} | all-to-all | bytes 256 | tf_op jit(solution)/shard_map/all_to_all | solution.py:118
  131.5 0.6 fusion.11
  133.5 0.1 fusion.8
  133.5 0.4 fusion
  134.0 34.1 %all_to_all.41 = bf16[128,8,512]{2,1,0:T(8,128)(2,1)S(1)} all-to-all(bf16[128,8,512]{2,1,0:T(8,128)(2,1)S(1)} %fusion), channel_id=1, replica_groups=mesh['ops_0'=4,'ops_1'=4,'ops_2'=8,'grp'=4] {'ops_0','ops_1','ops_2'}, dimensions={0} | all-to-all | bytes 2097152 | tf_op jit(solution)/shard_map/all_to_all | solution.py:112
  168.1 1.4 shard_map.79
  169.5 40.3 %all_to_all.42 = bf16[128,8,512]{2,1,0:T(8,128)(2,1)S(1)} all-to-all(bf16[128,8,512]{2,1,0:T(8,128)(2,1)S(1)} %bitcast.38), channel_id=1, replica_groups=mesh['ops_0'=4,'ops_1'=4,'ops_2'=8,'grp'=4] {'ops_0','ops_1','ops_2'}, dimensions={0} | all-to-all | bytes 2097152 | tf_op jit(solution)/shard_map/all_to_all | solution.py:112
  209.8 0.3 fusion.1
  210.1 0.7 copy.19
  210.8 6.8 %all-to-all-start.6 = ((bf16[4,128,128]{2,1,0:T(8,128)(2,1)}), bf16[4,128,128]{2,1,0:T(8,128)(2,1)S(1)}, u32[]{:S(2)}, u32[]{:S(2)}) async-start(bf16[4,128,128]{2,1,0:T(8,128)(2,1)} %bitcast.33), calls=%async_computation.6 | async-start | bytes 262144 | tf_op jit(solution)/shard_map/all_to_all | solution.py:153
  217.5 0.6 constant_dynamic-slice_fusion
  218.2 2.9 %all-to-all-done.6 = bf16[4,128,128]{2,1,0:T(8,128)(2,1)S(1)} async-done(((bf16[4,128,128]{2,1,0:T(8,128)(2,1)}), bf16[4,128,128]{2,1,0:T(8,128)(2,1)S(1)}, u32[]{:S(2)}, u32[]{:S(2)}) %all-to-all-start.6) | async-done | bytes 131104 | tf_op jit(solution)/shard_map/all_to_all | solution.py:153
  221.1 0.7 multiply_add_fusion
  (14 shorter events, 0.2 us)
Async XLA Ops:
  1.6 0.7 copy-start.2
  2.3 0.7 copy-start.3
  3.8 52.0 %copy-start = (bf16[1,512,512]{2,1,0:T(8,128)(2,1)S(1)}, bf16[1,512,512]{2,1,0:T(8,128)(2,1)}, u32[]{:S(2)}) copy-start(bf16[1,512,512]{2,1,0:T(8,128)(2,1)} %param.8) | copy-start | bytes 1572868
  3.8 52.0 %copy-start.1 = (bf16[1,512,512]{2,1,0:T(8,128)(2,1)S(1)}, bf16[1,512,512]{2,1,0:T(8,128)(2,1)}, u32[]{:S(2)}) copy-start(bf16[1,512,512]{2,1,0:T(8,128)(2,1)} %param.9) | copy-start | bytes 1572868
  94.7 9.9 %copy-start.5 = (f32[32,4,512]{2,1,0:T(4,128)S(1)}, f32[32,4,512]{2,1,0:T(4,128)}, u32[]{:S(2)}) copy-start(f32[32,4,512]{2,1,0:T(4,128)} %param.7) | copy-start | bytes 786436
  95.0 9.7 %copy-start.4 = (bf16[32,4,512]{2,1,0:T(4,128)(2,1)S(1)}, bf16[32,4,512]{2,1,0:T(4,128)(2,1)}, u32[]{:S(2)}) copy-start(bf16[32,4,512]{2,1,0:T(4,128)(2,1)} %param.6) | copy-start | bytes 393220
  95.0 6.7 %collective-permute-start = (f32[128,512]{1,0:T(8,128)S(1)}, f32[128,512]{1,0:T(8,128)S(1)}, u32[]{:S(2)}, u32[]{:S(2)}) collective-permute-start(f32[128,512]{1,0:T(8,128)S(1)} %fusion.3), channel_id=1, source_target_pairs={{0,1},{1,0},{2,3},{3,2},{4,5},{5,4},{6,7},{7,6},{8,9},{9,8},{10,11... | collective-permute-start | bytes 786440 | tf_op jit(solution)/shard_map/ppermute | solution.py:138
  101.8 6.6 %collective-permute-start.1 = (bf16[128,512]{1,0:T(8,128)(2,1)S(1)}, bf16[128,512]{1,0:T(8,128)(2,1)S(1)}, u32[]{:S(2)}, u32[]{:S(2)}) collective-permute-start(bf16[128,512]{1,0:T(8,128)(2,1)S(1)} %get-tuple-element.8), channel_id=1, source_target_pairs={{0,2},{1,3},{2,0},{3,1},{4,6},{5,7},{6,4},{7,5},{8,10},{9,11},{10,... | collective-permute-start | bytes 393224 | tf_op jit(solution)/shard_map/ppermute | solution.py:139
  210.8 10.3 %all-to-all-start.6 = ((bf16[4,128,128]{2,1,0:T(8,128)(2,1)}), bf16[4,128,128]{2,1,0:T(8,128)(2,1)S(1)}, u32[]{:S(2)}, u32[]{:S(2)}) async-start(bf16[4,128,128]{2,1,0:T(8,128)(2,1)} %bitcast.33), calls=%async_computation.6 | async-start | bytes 262144 | tf_op jit(solution)/shard_map/all_to_all | solution.py:153

commit v2 on v1

v2 whole, which is shorter than its diff:
```python
import functools

import jax
import jax.numpy as jnp
from jax import lax
from jax.experimental import pallas as pl
from jax.experimental.pallas import tpu as pltpu
from jax.sharding import Mesh
from jax.sharding import PartitionSpec as P

OPS = ("ops_0", "ops_1", "ops_2")
OPS_GRP = ("ops_0", "ops_1", "ops_2", "grp")
F32 = jnp.float32
BF16 = jnp.bfloat16
VMEM = pl.BlockSpec(memory_space=pltpu.VMEM)
CONTRACT_ROWS = (((0,), (0,)), ((), ()))
CONTRACT_COLUMNS = (((1,), (1,)), ((), ()))
LANES = 128


def iota(shape, dim):
    return lax.broadcasted_iota(jnp.int32, shape, dim)


def one_hot(mask):
    return jnp.where(mask, 1.0, 0.0).astype(BF16)


def whole(value):
    return value.astype(F32).astype(BF16)


def dot(left, right):
    return jnp.dot(left, right, preferred_element_type=F32)


def in_three(value):
    high = value.astype(BF16).astype(F32)
    middle = (value - high).astype(BF16).astype(F32)
    low = (value - high - middle).astype(BF16).astype(F32)
    return high, middle, low


def total(value):
    return jnp.sum(jnp.sum(value, axis=0, keepdims=True), axis=1, keepdims=True)


def select_kernel(groups, ends_ref, slot_ref, wave_ref, choose_ref, every_ref, out_ref):
    grp = lax.axis_index("grp")
    pairs = ends_ref.shape[1]
    ops = pairs // groups
    sectors = slot_ref.shape[1]
    rows_here = wave_ref.shape[0] // sectors
    messages = 2 * ops * rows_here
    ends = ends_ref[...]
    slot_row = whole(slot_ref[...])
    number = iota((sectors, pairs), 0)
    mine = one_hot(iota((pairs, ops), 0) == iota((pairs, ops), 1) * groups + grp)
    message = iota((ops, messages), 1) // rows_here
    holder = iota((ops, messages), 0) * 2
    row = (iota((1, messages), 1) % rows_here).astype(F32)
    places = iota((choose_ref.shape[0], messages), 0).astype(F32)
    slots = [
        dot(slot_row, one_hot(number == ends[end : end + 1])).astype(BF16) for end in range(2)
    ]
    spreads = [one_hot(message == holder + end) for end in range(2)]

    def chosen(first, second):
        wanted = (dot(first, spreads[0]) + dot(second, spreads[1])) * rows_here + row
        return one_hot(places == wanted)

    choose = chosen(*(dot(slot, mine).astype(BF16) for slot in slots))
    choose_ref[...] = choose
    out_ref[...] = lax.dot_general(
        choose, wave_ref[...], CONTRACT_ROWS, preferred_element_type=F32
    ).astype(BF16)
    for part in range(groups):
        held = slice(part * ops, (part + 1) * ops)
        every_ref[:, part * messages : (part + 1) * messages] = chosen(
            slots[0][:, held], slots[1][:, held]
        )


def pair_products(fetched_ref, left_ref, right_ref):
    block = left_ref.shape[0]
    width = right_ref.shape[0]
    tiles = block // 8
    fetched = fetched_ref[...].astype(F32).reshape(tiles, 2, 8, width)
    even, odd = fetched[:, 0], fetched[:, 1]
    upper = lax.broadcasted_iota(jnp.int32, even.shape, 1) < 4
    source = jnp.where(upper, even, pltpu.roll(odd, 4, 1)).reshape(block, width).astype(BF16)
    target = jnp.where(upper, pltpu.roll(even, 4, 1), odd).reshape(block, width).astype(BF16)
    left, right = left_ref[...], right_ref[...]
    inner = dot(left, source).astype(BF16)
    forward = dot(inner, right).reshape(tiles, 8, width)
    flipped = lax.dot_general(left, target, CONTRACT_ROWS, preferred_element_type=F32).astype(BF16)
    adjoint = lax.dot_general(
        flipped, right, CONTRACT_COLUMNS, preferred_element_type=F32
    ).reshape(tiles, 8, width)
    return (
        (even, odd),
        (
            jnp.where(upper, adjoint, pltpu.roll(forward, 4, 1)),
            jnp.where(upper, pltpu.roll(adjoint, 4, 1), forward),
        ),
    )


def first_pair_kernel(fetched_ref, left_ref, right_ref, wave_ref, diag_ref, out_ref):
    (even, odd), (out_even, out_odd) = pair_products(fetched_ref, left_ref, right_ref)
    width = right_ref.shape[0]
    rows = out_ref.shape[0]
    out_ref[:, :width] = (
        jnp.stack((out_even, out_odd), axis=1).reshape(rows, width).astype(BF16)
    )
    wave = wave_ref[...].astype(F32)
    sums = (
        total(jnp.sum(even * out_even + odd * out_odd, axis=0)),
        total(diag_ref[...] * wave * wave),
        total(wave * wave),
    )
    lane = iota((1, LANES), 1)
    carried = jnp.zeros((1, LANES), F32)
    for at, term in enumerate(term for value in sums for term in in_three(value)):
        carried = jnp.where(lane == at, term, carried)
    out_ref[:, width:] = jnp.broadcast_to(carried, (rows, LANES)).astype(BF16)


def second_pair_kernel(fetched_ref, left_ref, right_ref, out_ref):
    _, (out_even, out_odd) = pair_products(fetched_ref, left_ref, right_ref)
    for part in range(out_ref.shape[2]):
        held = slice(part * LANES, (part + 1) * LANES)
        out_ref[:, 0, part] = out_even[:, :, held].astype(BF16)
        out_ref[:, 1, part] = out_odd[:, :, held].astype(BF16)


def gather_kernel(choose_ref, arrived_ref, out_ref):
    rows = choose_ref.shape[0]
    width = out_ref.shape[1]
    out_ref[:rows, :] = dot(choose_ref[...], arrived_ref[:, :width])
    carried = jnp.sum(arrived_ref[:, width:].astype(F32), axis=0, keepdims=True) * 0.125
    out_ref[rows:, :] = jnp.zeros((8, width), F32)
    out_ref[rows:, :LANES] = jnp.broadcast_to(carried, (8, LANES))


def add_kernel(rows, own_ref, other_ref, sum_ref, half_ref):
    summed = own_ref[...] + other_ref[...]
    sum_ref[...] = summed
    half_ref[:rows, :] = summed[:rows].astype(BF16)
    high, middle, low = in_three(summed[rows:])
    place = iota(high.shape, 0)
    terms = jnp.where(place == 0, high, jnp.where(place == 1, middle, low))
    half_ref[rows:, :] = jnp.where(place < 3, terms, 0.0).astype(BF16)


def residual_kernel(
    groups, own_ref, other_ref, wave_ref, diag_ref, choose_ref, residual_ref, base_ref, out_ref
):
    grp = lax.axis_index("grp")
    rows = wave_ref.shape[0]
    share = residual_ref.shape[1]
    carried = own_ref[rows : rows + 1, :] + jnp.sum(
        other_ref[rows:, :].astype(F32), axis=0, keepdims=True
    )
    lane = iota(carried.shape, 1)
    pairs_part = total(jnp.where(lane < 3, carried, 0.0))
    diag_part = total(jnp.where((lane >= 3) & (lane < 6), carried, 0.0)) / groups
    square = total(jnp.where((lane >= 6) & (lane < 9), carried, 0.0)) / groups
    rayleigh = (pairs_part + diag_part) / square
    wave = wave_ref[...].astype(F32)
    applied = diag_ref[...] * wave + (own_ref[:rows, :] + other_ref[:rows, :].astype(F32))
    residual = applied - rayleigh * wave
    half = residual.astype(BF16)
    base = diag_ref[...] * half.astype(F32)
    for part in range(groups):

        @pl.when(grp == part)
        def _():
            residual_ref[...] = residual[:, part * share : (part + 1) * share]
            base_ref[...] = base[:, part * share : (part + 1) * share]

    out_ref[...] = lax.dot_general(
        choose_ref[...], half, CONTRACT_ROWS, preferred_element_type=F32
    ).astype(BF16)


def final_kernel(every_ref, arrived_ref, base_ref, out_ref):
    out_ref[...] = base_ref[...] + dot(every_ref[...], arrived_ref[...])


def call(kernel, outs, flops, *args):
    specs = jax.tree.map(lambda _: VMEM, outs)
    size = sum(arg.size * arg.dtype.itemsize for arg in args)
    return pl.pallas_call(
        kernel,
        out_shape=outs,
        in_specs=[VMEM] * len(args),
        out_specs=specs,
        compiler_params=pltpu.CompilerParams(vmem_limit_bytes=24 << 20),
        cost_estimate=pl.CostEstimate(flops=flops, bytes_accessed=2 * size, transcendentals=0),
    )(*args)


def array(shape, dtype):
    return jax.ShapeDtypeStruct(shape, dtype)


def exchange(value, axes):
    devices = lax.axis_size(axes)
    shaped = value.reshape(devices, -1, value.shape[-1])
    return lax.all_to_all(shaped, axes, 0, 0, tiled=True).reshape(-1, value.shape[-1])


def body(wave, diag_energy, left_ops, right_ops, pair_sectors, sector_slot):
    ops = lax.axis_size(OPS)
    groups = lax.axis_size("grp")
    sectors, rows_here, width = wave.shape
    rows = sectors * rows_here
    share = width // groups
    messages = 2 * ops * rows_here
    left, right = left_ops[0], right_ops[0]
    wave = wave.reshape(rows, width)
    diag = diag_energy.reshape(rows, width)
    choose, every, outgoing = call(
        functools.partial(select_kernel, groups),
        (
            array((rows, messages), BF16),
            array((rows, groups * messages), BF16),
            array((messages, width), BF16),
        ),
        400_000_000,
        pair_sectors.T,
        sector_slot[None],
        wave,
    )
    fetched = exchange(outgoing, OPS)
    blocks = call(
        first_pair_kernel,
        array((messages, width + LANES), BF16),
        1_100_000_000,
        fetched,
        left,
        right,
        wave,
        diag,
    )
    arrived = exchange(blocks, OPS)
    own = call(gather_kernel, array((rows + 8, width), F32), 150_000_000, choose, arrived)
    other = lax.ppermute(own, "grp", [(g, g ^ 1) for g in range(groups)])
    own, half = call(
        functools.partial(add_kernel, rows),
        (array(own.shape, F32), array(own.shape, BF16)),
        1_000_000,
        own,
        other,
    )
    other = lax.ppermute(half, "grp", [(g, g ^ 2) for g in range(groups)])
    residual, base, outgoing = call(
        functools.partial(residual_kernel, groups),
        (
            array((rows, share), F32),
            array((rows, share), F32),
            array((messages, width), BF16),
        ),
        150_000_000,
        own,
        other,
        wave,
        diag,
        choose,
    )
    fetched = exchange(outgoing, OPS)
    blocks = call(
        second_pair_kernel,
        array((ops // 2, 2, groups, 2 * rows_here, share), BF16),
        1_100_000_000,
        fetched,
        left,
        right,
    )
    arrived = exchange(blocks, OPS_GRP)
    sigma_out = call(final_kernel, array((rows, share), F32), 150_000_000, every, arrived, base)
    shape = (sectors, rows_here, share)
    return residual.reshape(shape), sigma_out.reshape(shape)


def solution(mesh):
    finer = Mesh(
        mesh.devices.reshape(4, 4, 8, mesh.shape["grp"]), ("ops_0", "ops_1", "ops_2", "grp")
    )
    return jax.shard_map(
        body,
        mesh=finer,
        in_specs=(
            P(None, OPS, None),
            P(None, OPS, None),
            P(OPS_GRP, None, None),
            P(OPS_GRP, None, None),
            P(),
            P(),
        ),
        out_specs=(P(None, OPS, "grp"), P(None, OPS, "grp")),
        check_vma=False,
    )
```

time: 222 us -> 202 us (0.910)
  blocking collectives: 185 us -> 126 us
  waiting for transfers between devices: 6.97 us -> 36.2 us
  starting transfers between devices: 15.2 us -> 28.9 us
  other arithmetic: 3.64 us -> 0 us
  Pallas kernels: 3.6 us -> 7.13 us
    all_to_all x6 -> x3, blocking collectives: 185 us -> 126 us  [exchange(): lax.all_to_all(shaped, axes, 0, 0, tiled=True).reshape(-1, value.shape[-1])]
    all_to_all x1, waiting for transfers between devices: 2.93 us -> 31.1 us  [exchange(): lax.all_to_all(shaped, axes, 0, 0, tiled=True).reshape(-1, value.shape[-1])]
    all_to_all x1, starting transfers between devices: 6.77 us -> 20.9 us  [exchange(): lax.all_to_all(shaped, axes, 0, 0, tiled=True).reshape(-1, value.shape[-1])]
    pallas_call x3 -> x7, Pallas kernels: 3.6 us -> 7.13 us  [call(): pl.pallas_call(kernel, out_shape=outs, in_specs=[VMEM] * len(args), out_s...]
  transfers between devices with their start and end apart: 3 -> 3, of which waited for: 3 -> 3; matrix products, arithmetic and copies ran while one was open for 1% -> 0% of each run, Pallas kernels for 0% -> 0%
where the time goes in v2:
time: 202 us
  blocking collectives  126 us (62%)
  waiting for transfers between devices  36.2 us (18%)
  starting transfers between devices  28.9 us (14%)
  Pallas kernels  7.13 us (4%)
  local copies, waits for them, and re-layouts  3.42 us (2%)
    all_to_all x3, blocking collectives, exchange(): lax.all_to_all(shaped, axes, 0, 0, tiled=True).reshape(-1, value.shape[-1])  126 us
    all_to_all x1, waiting for transfers between devices, exchange(): lax.all_to_all(shaped, axes, 0, 0, tiled=True).reshape(-1, value.shape[-1])  31.1 us
    all_to_all x1, starting transfers between devices, exchange(): lax.all_to_all(shaped, axes, 0, 0, tiled=True).reshape(-1, value.shape[-1])  20.9 us
    pallas_call x7, Pallas kernels, call(): pl.pallas_call(kernel, out_shape=outs, in_specs=[VMEM] * len(args), out_s...  7.13 us
    ppermute x1, starting transfers between devices, body(): other = lax.ppermute(own, 'grp', [(g, g ^ 1) for g in range(groups)])  5.1 us
  transfers between devices with their start and end apart: 3, of which 3 were waited for; matrix products, arithmetic and copies ran while one was open for 0% of the time, Pallas kernels for 0%

profile of v2, /device:TPU:1, one launch (start us, length us, event | category | flops | bytes accessed | tf_op | source)
XLA Modules:
  0.0 201.8 jit_solution(9692342488813174560)
XLA Ops:
  0.6 0.9 reshape.40.wave_ref
  1.6 0.0 copy-start.3
  1.6 0.7 copy-done.3
  2.3 0.0 copy-start.4
  2.3 0.7 copy-done.4
  2.9 1.8 shard_map.77
  4.8 0.0 copy-start.5
  4.8 0.0 copy-start
  4.8 20.9 %all-to-all-start = ((bf16[128,8,512]{2,1,0:T(8,128)(2,1)}), bf16[128,8,512]{2,1,0:T(8,128)(2,1)S(1)}, u32[]{:S(2)}, u32[]{:S(2)}) async-start(bf16[128,8,512]{2,1,0:T(8,128)(2,1)} %bitcast.2), calls=%async_computation | async-start | bytes 2097152 | tf_op jit(solution)/shard_map/all_to_all | solution.py:211
  25.7 0.0 copy-done.5
  25.7 0.1 reshape.43.diag_ref
  25.8 31.1 %all-to-all-done = bf16[128,8,512]{2,1,0:T(8,128)(2,1)S(1)} async-done(((bf16[128,8,512]{2,1,0:T(8,128)(2,1)}), bf16[128,8,512]{2,1,0:T(8,128)(2,1)S(1)}, u32[]{:S(2)}, u32[]{:S(2)}) %all-to-all-start) | async-done | bytes 1048608 | tf_op jit(solution)/shard_map/all_to_all | solution.py:211
  56.9 0.0 copy-done
  56.9 0.0 copy-start.1
  56.9 1.0 copy-done.1
  57.9 1.7 shard_map.78
  59.6 43.5 %all_to_all.20 = bf16[128,8,640]{2,1,0:T(8,128)(2,1)S(1)} all-to-all(bf16[128,8,640]{2,1,0:T(8,128)(2,1)S(1)} %bitcast.16), channel_id=1, replica_groups=mesh['ops_0'=4,'ops_1'=4,'ops_2'=8,'grp'=4] {'ops_0','ops_1','ops_2'}, dimensions={0} | all-to-all | bytes 2621440 | tf_op jit(solution)/shard_map/all_to_all | solution.py:211
  103.1 0.3 shard_map.79.own_ref
  103.4 5.1 %collective-permute-start = (f32[136,512]{1,0:T(8,128)S(1)}, f32[136,512]{1,0:T(8,128)S(1)}, u32[]{:S(2)}, u32[]{:S(2)}) collective-permute-start(f32[136,512]{1,0:T(8,128)S(1)} %shard_map.79.own_ref), channel_id=1, source_target_pairs={{0,1},{1,0},{2,3},{3,2},{4,5},{5,4},{6,7},{7,6},{8,9},{9,8},{10,11... | collective-permute-start | bytes 835592 | tf_op jit(solution)/shard_map/ppermute | solution.py:249
  108.6 1.2 collective-permute-done.other_ref
  109.8 2.8 %collective-permute-start.1 = (bf16[136,512]{1,0:T(8,128)(2,1)S(1)}, bf16[136,512]{1,0:T(8,128)(2,1)S(1)}, u32[]{:S(2)}, u32[]{:S(2)}) collective-permute-start(bf16[136,512]{1,0:T(8,128)(2,1)S(1)} %get-tuple-element.13), channel_id=1, source_target_pairs={{0,2},{1,3},{2,0},{3,1},{4,6},{5,7},{6,4},{7,5},{8,10},{9,11},{10,... | collective-permute-start | bytes 417800 | tf_op jit(solution)/shard_map/ppermute | solution.py:257
  112.6 3.9 %collective-permute-done.1.other_ref = bf16[136,512]{1,0:T(8,128)(2,1)S(1)} collective-permute-done((bf16[136,512]{1,0:T(8,128)(2,1)S(1)}, bf16[136,512]{1,0:T(8,128)(2,1)S(1)}, u32[]{:S(2)}, u32[]{:S(2)}) %collective-permute-start.1) | collective-permute-done | bytes 139296 | tf_op jit(solution)/shard_map/ppermute | solution.py:257
  116.5 0.8 shard_map.81
  117.3 0.0 copy-start.2
  117.3 37.1 %all_to_all.21 = bf16[128,8,512]{2,1,0:T(8,128)(2,1)S(1)} all-to-all(bf16[128,8,512]{2,1,0:T(8,128)(2,1)S(1)} %bitcast.18), channel_id=1, replica_groups=mesh['ops_0'=4,'ops_1'=4,'ops_2'=8,'grp'=4] {'ops_0','ops_1','ops_2'}, dimensions={0} | all-to-all | bytes 2097152 | tf_op jit(solution)/shard_map/all_to_all | solution.py:211
  154.5 0.0 copy-done.2
  154.5 1.4 shard_map.82
  155.9 44.9 %all_to_all.22 = bf16[512,8,128]{2,1,0:T(8,128)(2,1)S(1)} all-to-all(bf16[512,8,128]{2,1,0:T(8,128)(2,1)S(1)} %bitcast.20), channel_id=1, replica_groups=mesh['ops_0'=4,'ops_1'=4,'ops_2'=8,'grp'=4] {'ops_0','ops_1','ops_2','grp'}, dimensions={0} | all-to-all | bytes 2097152 | tf_op jit(solution)/shard_map/all_to_all | solution.py:211
  200.8 1.1 shard_map.83
  (1 shorter events, 0.0 us)
Async XLA Ops:
  1.6 0.7 copy-start.3
  2.3 0.7 copy-start.4
  4.8 20.9 %copy-start.5 = (f32[32,4,512]{2,1,0:T(4,128)S(1)}, f32[32,4,512]{2,1,0:T(4,128)}, u32[]{:S(2)}) copy-start(f32[32,4,512]{2,1,0:T(4,128)} %param.7) | copy-start | bytes 786436
  4.8 52.1 %copy-start = (bf16[1,512,512]{2,1,0:T(8,128)(2,1)S(1)}, bf16[1,512,512]{2,1,0:T(8,128)(2,1)}, u32[]{:S(2)}) copy-start(bf16[1,512,512]{2,1,0:T(8,128)(2,1)} %param.8) | copy-start | bytes 1572868
  4.8 52.1 %all-to-all-start = ((bf16[128,8,512]{2,1,0:T(8,128)(2,1)}), bf16[128,8,512]{2,1,0:T(8,128)(2,1)S(1)}, u32[]{:S(2)}, u32[]{:S(2)}) async-start(bf16[128,8,512]{2,1,0:T(8,128)(2,1)} %bitcast.2), calls=%async_computation | async-start | bytes 2097152 | tf_op jit(solution)/shard_map/all_to_all | solution.py:211
  56.9 1.0 copy-start.1
  103.4 6.3 %collective-permute-start = (f32[136,512]{1,0:T(8,128)S(1)}, f32[136,512]{1,0:T(8,128)S(1)}, u32[]{:S(2)}, u32[]{:S(2)}) collective-permute-start(f32[136,512]{1,0:T(8,128)S(1)} %shard_map.79.own_ref), channel_id=1, source_target_pairs={{0,1},{1,0},{2,3},{3,2},{4,5},{5,4},{6,7},{7,6},{8,9},{9,8},{10,11... | collective-permute-start | bytes 835592 | tf_op jit(solution)/shard_map/ppermute | solution.py:249
  109.8 6.8 %collective-permute-start.1 = (bf16[136,512]{1,0:T(8,128)(2,1)S(1)}, bf16[136,512]{1,0:T(8,128)(2,1)S(1)}, u32[]{:S(2)}, u32[]{:S(2)}) collective-permute-start(bf16[136,512]{1,0:T(8,128)(2,1)S(1)} %get-tuple-element.13), channel_id=1, source_target_pairs={{0,2},{1,3},{2,0},{3,1},{4,6},{5,7},{6,4},{7,5},{8,10},{9,11},{10,... | collective-permute-start | bytes 417800 | tf_op jit(solution)/shard_map/ppermute | solution.py:257
  117.3 37.1 %copy-start.2 = (bf16[1,512,512]{2,1,0:T(8,128)(2,1)S(1)}, bf16[1,512,512]{2,1,0:T(8,128)(2,1)}, u32[]{:S(2)}) copy-start(bf16[1,512,512]{2,1,0:T(8,128)(2,1)} %param.9) | copy-start | bytes 1572868

commit v3 on v2

v3 whole, which is shorter than its diff:
```python
import functools

import jax
import jax.numpy as jnp
from jax import lax
from jax.experimental import pallas as pl
from jax.experimental.pallas import tpu as pltpu
from jax.sharding import Mesh
from jax.sharding import PartitionSpec as P

OPS = ("ops_0", "ops_1", "ops_2", "ops_3")
OPS_GRP = (*OPS, "grp")
NEAR = ("ops_0", "ops_3", "grp")
FAR = ("ops_1", "ops_2")
F32 = jnp.float32
BF16 = jnp.bfloat16
VMEM = pl.BlockSpec(memory_space=pltpu.VMEM)
CONTRACT_ROWS = (((0,), (0,)), ((), ()))
CONTRACT_COLUMNS = (((1,), (1,)), ((), ()))


def iota(shape, dim):
    return lax.broadcasted_iota(jnp.int32, shape, dim)


def one_hot(mask):
    return jnp.where(mask, 1.0, 0.0).astype(BF16)


def whole(value):
    return value.astype(F32).astype(BF16)


def dot(left, right):
    return jnp.dot(left, right, preferred_element_type=F32)


def in_three(value):
    high = value.astype(BF16).astype(F32)
    middle = (value - high).astype(BF16).astype(F32)
    low = (value - high - middle).astype(BF16).astype(F32)
    return high, middle, low


def total(value):
    return jnp.sum(jnp.sum(value, axis=0, keepdims=True), axis=1, keepdims=True)


def select_kernel(
    groups, inner, ends_ref, slot_ref, wave_ref, near_ref, every_ref, out_ref
):
    grp = lax.axis_index("grp")
    far = lax.axis_index("ops_1") * lax.axis_size("ops_2") + lax.axis_index("ops_2")
    far_count = lax.axis_size("ops_1") * lax.axis_size("ops_2")
    pairs = ends_ref.shape[1]
    ops = pairs // groups
    sectors = slot_ref.shape[1]
    rows = wave_ref.shape[0]
    rows_here = rows // sectors
    ends = ends_ref[...]
    slot_row = whole(slot_ref[...])
    number = iota((sectors, pairs), 0)
    slots = [
        dot(slot_row, one_hot(number == ends[end : end + 1])).astype(BF16) for end in range(2)
    ]

    def spreads_of(count):
        shape = (count, 2 * count * rows_here)
        message = iota(shape, 1) // rows_here
        return [one_hot(message == iota(shape, 0) * 2 + end) for end in range(2)]

    def chosen(slots, spreads):
        messages = spreads[0].shape[1]
        row = (iota((1, messages), 1) % rows_here).astype(F32)
        wanted = sum(dot(slot, spread) for slot, spread in zip(slots, spreads)) * rows_here + row
        return one_hot(iota((rows, messages), 0).astype(F32) == wanted)

    spreads = spreads_of(ops)
    mine = one_hot(iota((pairs, ops), 0) == iota((pairs, ops), 1) * groups + grp)
    choose = chosen([dot(slot, mine).astype(BF16) for slot in slots], spreads)
    out_ref[...] = lax.dot_general(
        choose, wave_ref[...], CONTRACT_ROWS, preferred_element_type=F32
    ).astype(BF16)
    messages = choose.shape[1]
    for part in range(groups):
        held = slice(part * ops, (part + 1) * ops)
        every_ref[:, part * messages : (part + 1) * messages] = chosen(
            [slot[:, held] for slot in slots], spreads
        )
    near_count = pairs // far_count
    member = iota((pairs, near_count), 1)
    pair = (member // inner * far_count + far) * inner + member % inner
    near = one_hot(iota((pairs, near_count), 0) == pair)
    near_ref[...] = chosen(
        [dot(slot, near).astype(BF16) for slot in slots], spreads_of(near_count)
    )


def pair_products(even, odd, left_ref, right_ref, right_copy):
    block = left_ref.shape[0]
    tiles, _, width = even.shape
    upper = lax.broadcasted_iota(jnp.int32, even.shape, 1) < 4
    source = jnp.where(upper, even, pltpu.roll(odd, 4, 1)).reshape(block, width).astype(BF16)
    target = jnp.where(upper, pltpu.roll(even, 4, 1), odd).reshape(block, width).astype(BF16)
    left = left_ref[...]
    inner = dot(left, source).astype(BF16)
    flipped = lax.dot_general(left, target, CONTRACT_ROWS, preferred_element_type=F32).astype(BF16)
    right_copy.wait()
    right = right_ref[...]
    forward = dot(inner, right).reshape(tiles, 8, width)
    adjoint = lax.dot_general(
        flipped, right, CONTRACT_COLUMNS, preferred_element_type=F32
    ).reshape(tiles, 8, width)
    return (
        jnp.where(upper, adjoint, pltpu.roll(forward, 4, 1)),
        jnp.where(upper, pltpu.roll(adjoint, 4, 1), forward),
    )


def first_pair_kernel(
    fetched_ref, left_ref, right_hbm, wave_ref, diag_ref, out_ref, right_ref, done
):
    copy = pltpu.make_async_copy(right_hbm, right_ref, done)
    copy.start()
    width = right_ref.shape[0]
    tiles = left_ref.shape[0] // 8
    blocks, _, groups, slots, _, share = out_ref.shape
    far = slots - 1
    fetched = fetched_ref[...].astype(F32).reshape(tiles, 2, 8, width)
    even, odd = fetched[:, 0], fetched[:, 1]
    products = pair_products(even, odd, left_ref, right_ref, copy)
    for block in range(blocks):
        for parity, product in enumerate(products):
            for grp in range(groups):
                out_ref[block, parity, grp, :far] = product[
                    block * far : (block + 1) * far, :, grp * share : (grp + 1) * share
                ].astype(BF16)
    wave = wave_ref[...].astype(F32)
    sums = (
        total(jnp.sum(even * products[0] + odd * products[1], axis=0)),
        total(diag_ref[...] * wave * wave),
        total(wave * wave),
    )
    lane = iota((1, share), 1)
    carried = jnp.zeros((1, share), F32)
    for at, term in enumerate(term for value in sums for term in in_three(value)):
        carried = jnp.where(lane == at, term, carried)
    carried = jnp.broadcast_to(carried, (8, share)).astype(BF16)
    for block in range(blocks):
        for parity in range(2):
            for grp in range(groups):
                out_ref[block, parity, grp, far] = carried


def second_pair_kernel(fetched_ref, left_ref, right_hbm, out_ref, right_ref, done):
    copy = pltpu.make_async_copy(right_hbm, right_ref, done)
    copy.start()
    groups, share = fetched_ref.shape[2], fetched_ref.shape[4]
    even, odd = (
        jnp.concatenate(
            [fetched_ref[:, parity, grp].astype(F32) for grp in range(groups)], axis=2
        )
        for parity in range(2)
    )
    products = pair_products(even, odd, left_ref, right_ref, copy)
    for parity, product in enumerate(products):
        for grp in range(groups):
            out_ref[:, parity, grp] = product[:, :, grp * share : (grp + 1) * share].astype(BF16)


def gather_kernel(near_ref, arrived_ref, out_ref):
    members, slots, _, share = arrived_ref.shape
    far = slots - 1
    rows = near_ref.shape[0]
    near = near_ref[...]
    carried = jnp.sum(arrived_ref[:, far].astype(F32), axis=0)
    high, middle, low = in_three(carried)
    place = iota(carried.shape, 0)
    terms = jnp.where(place == 0, high, jnp.where(place == 1, middle, low))
    terms = jnp.where(place < 3, terms, 0.0).astype(BF16)
    for at in range(far):
        arrived = arrived_ref[:, at].reshape(members * 8, share)
        out_ref[at, :rows] = dot(near, arrived).astype(BF16)
        out_ref[at, rows:] = terms


def residual_kernel(groups, arrived_ref, wave_ref, diag_ref, every_ref, residual_ref, base_ref, out_ref):
    rows, share = residual_ref.shape
    arrived = jnp.sum(arrived_ref[...].astype(F32), axis=0)
    carried = jnp.sum(arrived[rows:], axis=0, keepdims=True)
    lane = iota(carried.shape, 1)
    pairs_part = total(jnp.where(lane < 3, carried, 0.0))
    diag_part = total(jnp.where((lane >= 3) & (lane < 6), carried, 0.0)) / groups
    square = total(jnp.where((lane >= 6) & (lane < 9), carried, 0.0)) / groups
    rayleigh = (pairs_part + diag_part) / square
    mine = pl.ds(pl.multiple_of(lax.axis_index("grp") * share, share), share)
    wave = wave_ref[:, mine].astype(F32)
    diag = diag_ref[:, mine]
    residual = diag * wave + arrived[:rows] - rayleigh * wave
    half = residual.astype(BF16)
    residual_ref[...] = residual
    base_ref[...] = diag * half.astype(F32)
    out_ref[...] = lax.dot_general(
        every_ref[...], half, CONTRACT_ROWS, preferred_element_type=F32
    ).astype(BF16)


def final_kernel(every_ref, arrived_ref, base_ref, out_ref):
    out_ref[...] = base_ref[...] + dot(every_ref[...], arrived_ref[...])


def call(kernel, outs, flops, *args, scratch=(), far_away=()):
    specs = jax.tree.map(lambda _: VMEM, outs)
    size = sum(arg.size * arg.dtype.itemsize for arg in args)
    return pl.pallas_call(
        kernel,
        out_shape=outs,
        in_specs=[
            pl.BlockSpec(memory_space=pltpu.HBM) if at in far_away else VMEM
            for at in range(len(args))
        ],
        out_specs=specs,
        scratch_shapes=scratch,
        compiler_params=pltpu.CompilerParams(vmem_limit_bytes=24 << 20),
        cost_estimate=pl.CostEstimate(flops=flops, bytes_accessed=2 * size, transcendentals=0),
    )(*args)


def array(shape, dtype):
    return jax.ShapeDtypeStruct(shape, dtype)


def exchange(value, axes):
    return lax.all_to_all(value, axes, 0, 0, tiled=True)


def body(wave, diag_energy, left_ops, right_ops, pair_sectors, sector_slot):
    ops = lax.axis_size(OPS)
    groups = lax.axis_size("grp")
    far = lax.axis_size(FAR)
    near = lax.axis_size(NEAR)
    blocks = lax.axis_size("ops_0")
    sectors, rows_here, width = wave.shape
    rows = sectors * rows_here
    share = width // groups
    messages = 2 * ops * rows_here
    left, right = left_ops[0], right_ops[0]
    wave = wave.reshape(rows, width)
    diag = diag_energy.reshape(rows, width)
    held = (pltpu.VMEM(right.shape, BF16), pltpu.SemaphoreType.DMA)
    near_choose, every, outgoing = call(
        functools.partial(select_kernel, groups, near // blocks),
        (
            array((rows, 2 * near * rows_here), BF16),
            array((rows, groups * messages), BF16),
            array((messages, width), BF16),
        ),
        400_000_000,
        pair_sectors.T,
        sector_slot[None],
        wave,
    )
    fetched = exchange(outgoing.reshape(ops, -1, width), OPS).reshape(messages, width)
    scattered = call(
        first_pair_kernel,
        array((blocks, 2, groups, far + 1, 8, share), BF16),
        1_100_000_000,
        fetched,
        left,
        right,
        wave,
        diag,
        scratch=held,
        far_away=(2,),
    )
    arrived = exchange(scattered.reshape(near, far + 1, 8, share), NEAR)
    partial = call(
        gather_kernel, array((far, rows + 8, share), BF16), 150_000_000, near_choose, arrived
    )
    arrived = exchange(partial, FAR)
    residual, base, outgoing = call(
        functools.partial(residual_kernel, groups),
        (
            array((rows, share), F32),
            array((rows, share), F32),
            array((groups * messages, share), BF16),
        ),
        150_000_000,
        arrived,
        wave,
        diag,
        every,
    )
    fetched = exchange(outgoing.reshape(ops * groups, -1, share), OPS_GRP)
    shape = (ops // 2, 2, groups, 2 * rows_here, share)
    scattered = call(
        second_pair_kernel,
        array(shape, BF16),
        1_100_000_000,
        fetched.reshape(shape),
        left,
        right,
        scratch=held,
        far_away=(2,),
    )
    arrived = exchange(scattered.reshape(ops * groups, -1, share), OPS_GRP)
    sigma_out = call(
        final_kernel,
        array((rows, share), F32),
        150_000_000,
        every,
        arrived.reshape(groups * messages, share),
        base,
    )
    shape = (sectors, rows_here, share)
    return residual.reshape(shape), sigma_out.reshape(shape)


def solution(mesh):
    finer = Mesh(mesh.devices.reshape(4, 4, 4, 2, mesh.shape["grp"]), OPS_GRP)
    return jax.shard_map(
        body,
        mesh=finer,
        in_specs=(
            P(None, OPS, None),
            P(None, OPS, None),
            P(OPS_GRP, None, None),
            P(OPS_GRP, None, None),
            P(),
            P(),
        ),
        out_specs=(P(None, OPS, "grp"), P(None, OPS, "grp")),
        check_vma=False,
    )
```

time: 202 us -> 201 us (level)
  blocking collectives: 126 us -> 136 us
  starting transfers between devices: 28.9 us -> 20.9 us
  waiting for transfers between devices: 36.2 us -> 31.1 us
    all_to_all x3 -> x4, blocking collectives: 126 us -> 136 us  [exchange(): return lax.all_to_all(value, axes, 0, 0, tiled=True)]
    ppermute x2 -> x0, starting transfers between devices: 7.93 us -> none  [the longest x1 5.1 us: body(): other = lax.ppermute(own, 'grp', [(g, g ^ 1) for g in range(groups)])]
    ppermute x2 -> x0, waiting for transfers between devices: 5.08 us -> none  [the longest x1 3.92 us: body(): other = lax.ppermute(half, 'grp', [(g, g ^ 2) for g in range(groups)])]
    pallas_call x7 -> x6, Pallas kernels: 7.13 us -> 7.94 us  [call(): pl.pallas_call(kernel, out_shape=outs, in_specs=[pl.BlockSpec(memory_spac...]
  transfers between devices with their start and end apart: 3 -> 1, of which waited for: 3 -> 1; matrix products, arithmetic and copies ran while one was open for 0% -> 0% of each run, Pallas kernels for 0% -> 0%
where the time goes in v3:
time: 201 us; the launch traced here: 200 us
  blocking collectives  136 us (68%)
  waiting for transfers between devices  31.1 us (15%)
  starting transfers between devices  20.9 us (10%)
  Pallas kernels  7.94 us (4%)
  local copies, waits for them, and re-layouts  3.42 us (2%)
    all_to_all x4, blocking collectives, exchange(): return lax.all_to_all(value, axes, 0, 0, tiled=True)  136 us
    all_to_all x1, waiting for transfers between devices, exchange(): return lax.all_to_all(value, axes, 0, 0, tiled=True)  31.1 us
    all_to_all x1, starting transfers between devices, exchange(): return lax.all_to_all(value, axes, 0, 0, tiled=True)  20.9 us
    pallas_call x6, Pallas kernels, call(): pl.pallas_call(kernel, out_shape=outs, in_specs=[pl.BlockSpec(memory_spac...  7.94 us
  transfers between devices with their start and end apart: 1, of which 1 were waited for; matrix products, arithmetic and copies ran while one was open for 0% of the time, Pallas kernels for 0%

profile of v3, /device:TPU:1, one launch (start us, length us, event | category | flops | bytes accessed | tf_op | source)
XLA Modules:
  0.0 200.2 jit_solution(11743800834123907874)
XLA Ops:
  0.6 0.9 reshape.37.wave_ref
  1.6 0.0 copy-start.3
  1.6 0.7 copy-done.3
  2.3 0.0 copy-start.4
  2.3 0.7 copy-done.4
  2.9 2.2 %shard_map.77 = (bf16[128,256]{1,0:T(8,128)(2,1)S(1)}, bf16[128,4096]{1,0:T(8,128)(2,1)S(1)}, bf16[1024,512]{1,0:T(8,128)(2,1)}) custom-call(s32[2,512]{1,0:T(2,128)S(1)} %bitcast.23, s32[1,32]{1,0:T(1,128)S(1)} %bitcast.24, bf16[128,512]{1,0:T(8,128)(2,1)S(1)} %reshape.37.wave_ref), custom_call_target="tpu_custom_call" | custom-call | flops 400000000 | bytes 270592 | tf_op jit(solution)/shard_map/pallas_call | solution.py:215
  5.1 0.0 copy-start.5
  5.1 0.0 copy-start
  5.1 20.9 %all-to-all-start = ((bf16[128,8,512]{2,1,0:T(8,128)(2,1)}), bf16[128,8,512]{2,1,0:T(8,128)(2,1)S(1)}, u32[]{:S(2)}, u32[]{:S(2)}) async-start(bf16[128,8,512]{2,1,0:T(8,128)(2,1)} %bitcast.2), calls=%async_computation | async-start | bytes 2097152 | tf_op jit(solution)/shard_map/all_to_all | solution.py:234
  26.0 0.0 copy-done.5
  26.1 0.1 reshape.40.diag_ref
  26.2 31.1 %all-to-all-done = bf16[128,8,512]{2,1,0:T(8,128)(2,1)S(1)} async-done(((bf16[128,8,512]{2,1,0:T(8,128)(2,1)}), bf16[128,8,512]{2,1,0:T(8,128)(2,1)S(1)}, u32[]{:S(2)}, u32[]{:S(2)}) %all-to-all-start) | async-done | bytes 1048608 | tf_op jit(solution)/shard_map/all_to_all | solution.py:234
  57.2 0.0 copy-done
  57.2 0.0 copy-start.1
  57.2 1.0 copy-done.1
  58.3 1.9 shard_map.78
  60.1 23.2 %all_to_all.25.arrived_ref = bf16[32,17,8,128]{3,2,1,0:T(8,128)(2,1)S(1)} all-to-all(bf16[32,17,8,128]{3,2,1,0:T(8,128)(2,1)S(1)} %bitcast.14), channel_id=1, replica_groups=mesh['ops_0'=4,'ops_1'=4,'ops_2'=4,'ops_3'=2,'grp'=4] {'ops_0','ops_3','..., dimensions={0} | all-to-all | bytes 2228224 | tf_op jit(solution)/shard_map/all_to_all | solution.py:234
  83.3 0.4 shard_map.79
  83.7 24.7 %all_to_all.26.arrived_ref = bf16[16,136,128]{2,1,0:T(8,128)(2,1)S(1)} all-to-all(bf16[16,136,128]{2,1,0:T(8,128)(2,1)S(1)} %shard_map.79), channel_id=1, replica_groups=mesh['ops_0'=4,'ops_1'=4,'ops_2'=4,'ops_3'=2,'grp'=4] {'ops_1','ops_2'}, dimensions={0} | all-to-all | bytes 1114112 | tf_op jit(solution)/shard_map/all_to_all | solution.py:234
  108.4 0.8 shard_map.80
  109.2 0.0 copy-start.2
  109.2 44.6 %all_to_all.27 = bf16[512,8,128]{2,1,0:T(8,128)(2,1)S(1)} all-to-all(bf16[512,8,128]{2,1,0:T(8,128)(2,1)S(1)} %bitcast.16), channel_id=1, replica_groups=mesh['ops_0'=4,'ops_1'=4,'ops_2'=4,'ops_3'=2,'grp'=4] {'ops_0','ops_1','..., dimensions={0} | all-to-all | bytes 2097152 | tf_op jit(solution)/shard_map/all_to_all | solution.py:234
  153.8 0.0 copy-done.2
  153.8 1.7 shard_map.81
  155.5 43.6 %all_to_all.28 = bf16[512,8,128]{2,1,0:T(8,128)(2,1)S(1)} all-to-all(bf16[512,8,128]{2,1,0:T(8,128)(2,1)S(1)} %bitcast.18), channel_id=1, replica_groups=mesh['ops_0'=4,'ops_1'=4,'ops_2'=4,'ops_3'=2,'grp'=4] {'ops_0','ops_1','..., dimensions={0} | all-to-all | bytes 2097152 | tf_op jit(solution)/shard_map/all_to_all | solution.py:234
  199.1 1.1 shard_map.82
Async XLA Ops:
  1.6 0.7 copy-start.3
  2.3 0.7 copy-start.4
  5.1 20.9 %copy-start.5 = (f32[32,4,512]{2,1,0:T(4,128)S(1)}, f32[32,4,512]{2,1,0:T(4,128)}, u32[]{:S(2)}) copy-start(f32[32,4,512]{2,1,0:T(4,128)} %param.7) | copy-start | bytes 786436
  5.1 52.1 %copy-start = (bf16[1,512,512]{2,1,0:T(8,128)(2,1)S(1)}, bf16[1,512,512]{2,1,0:T(8,128)(2,1)}, u32[]{:S(2)}) copy-start(bf16[1,512,512]{2,1,0:T(8,128)(2,1)} %param.8) | copy-start | bytes 1572868
  5.1 52.1 %all-to-all-start = ((bf16[128,8,512]{2,1,0:T(8,128)(2,1)}), bf16[128,8,512]{2,1,0:T(8,128)(2,1)S(1)}, u32[]{:S(2)}, u32[]{:S(2)}) async-start(bf16[128,8,512]{2,1,0:T(8,128)(2,1)} %bitcast.2), calls=%async_computation | async-start | bytes 2097152 | tf_op jit(solution)/shard_map/all_to_all | solution.py:234
  57.2 1.0 copy-start.1
  109.2 44.6 %copy-start.2 = (bf16[1,512,512]{2,1,0:T(8,128)(2,1)S(1)}, bf16[1,512,512]{2,1,0:T(8,128)(2,1)}, u32[]{:S(2)}) copy-start(bf16[1,512,512]{2,1,0:T(8,128)(2,1)} %param.9) | copy-start | bytes 1572868

commit v4 on v3

--- a/solution.py
+++ b/solution.py
@@ -46,57 +46,71 @@
     return jnp.sum(jnp.sum(value, axis=0, keepdims=True), axis=1, keepdims=True)
 
 
-def select_kernel(
-    groups, inner, ends_ref, slot_ref, wave_ref, near_ref, every_ref, out_ref
-):
+def spreads_of(count, rows_here):
+    shape = (count, 2 * count * rows_here)
+    message = iota(shape, 1) // rows_here
+    return [one_hot(message == iota(shape, 0) * 2 + end) for end in range(2)]
+
+
+def chosen(slots, spreads, rows, rows_here):
+    messages = spreads[0].shape[1]
+    row = (iota((1, messages), 1) % rows_here).astype(F32)
+    wanted = sum(dot(slot, spread) for slot, spread in zip(slots, spreads)) * rows_here + row
+    return one_hot(iota((rows, messages), 0).astype(F32) == wanted)
+
+
+def slots_of(ends_ref, slot_ref):
+    ends = ends_ref[...]
+    slot_row = whole(slot_ref[...])
+    number = iota((slot_row.shape[1], ends.shape[1]), 0)
+    return [
+        dot(slot_row, one_hot(number == ends[end : end + 1])).astype(BF16) for end in range(2)
+    ]
+
+
+def select_kernel(groups, ends_ref, slot_ref, wave_ref, out_ref):
     grp = lax.axis_index("grp")
+    pairs = ends_ref.shape[1]
+    ops = pairs // groups
+    sectors, rows_here, width = wave_ref.shape
+    rows = sectors * rows_here
+    mine = one_hot(iota((pairs, ops), 0) == iota((pairs, ops), 1) * groups + grp)
+    slots = [dot(slot, mine).astype(BF16) for slot in slots_of(ends_ref, slot_ref)]
+    choose = chosen(slots, spreads_of(ops, rows_here), rows, rows_here)
+    wave = wave_ref[...].astype(F32).reshape(rows, width).astype(BF16)
+    out_ref[...] = lax.dot_general(
+        choose, wave, CONTRACT_ROWS, preferred_element_type=F32
+    ).astype(BF16)
+
+
+def table_kernel(groups, inner, ends_ref, slot_ref, near_ref, every_ref):
     far = lax.axis_index("ops_1") * lax.axis_size("ops_2") + lax.axis_index("ops_2")
     far_count = lax.axis_size("ops_1") * lax.axis_size("ops_2")
     pairs = ends_ref.shape[1]
     ops = pairs // groups
-    sectors = slot_ref.shape[1]
-    rows = wave_ref.shape[0]
-    rows_here = rows // sectors
-    ends = ends_ref[...]
-    slot_row = whole(slot_ref[...])
-    number = iota((sectors, pairs), 0)
-    slots = [
-        dot(slot_row, one_hot(number == ends[end : end + 1])).astype(BF16) for end in range(2)
-    ]
-
-    def spreads_of(count):
-        shape = (count, 2 * count * rows_here)
-        message = iota(shape, 1) // rows_here
-        return [one_hot(message == iota(shape, 0) * 2 + end) for end in range(2)]
-
-    def chosen(slots, spreads):
-        messages = spreads[0].shape[1]
-        row = (iota((1, messages), 1) % rows_here).astype(F32)
-        wanted = sum(dot(slot, spread) for slot, spread in zip(slots, spreads)) * rows_here + row
-        return one_hot(iota((rows, messages), 0).astype(F32) == wanted)
-
-    spreads = spreads_of(ops)
-    mine = one_hot(iota((pairs, ops), 0) == iota((pairs, ops), 1) * groups + grp)
-    choose = chosen([dot(slot, mine).astype(BF16) for slot in slots], spreads)
-    out_ref[...] = lax.dot_general(
-        choose, wave_ref[...], CONTRACT_ROWS, preferred_element_type=F32
-    ).astype(BF16)
-    messages = choose.shape[1]
+    rows = near_ref.shape[0]
+    rows_here = rows // slot_ref.shape[1]
+    slots = slots_of(ends_ref, slot_ref)
+    spreads = spreads_of(ops, rows_here)
+    messages = 2 * ops * rows_here
     for part in range(groups):
         held = slice(part * ops, (part + 1) * ops)
         every_ref[:, part * messages : (part + 1) * messages] = chosen(
-            [slot[:, held] for slot in slots], spreads
+            [slot[:, held] for slot in slots], spreads, rows, rows_here
         )
     near_count = pairs // far_count
     member = iota((pairs, near_count), 1)
     pair = (member // inner * far_count + far) * inner + member % inner
     near = one_hot(iota((pairs, near_count), 0) == pair)
     near_ref[...] = chosen(
-        [dot(slot, near).astype(BF16) for slot in slots], spreads_of(near_count)
-    )
-
-
-def pair_products(even, odd, left_ref, right_ref, right_copy):
+        [dot(slot, near).astype(BF16) for slot in slots],
+        spreads_of(near_count, rows_here),
+        rows,
+        rows_here,
+    )
+
+
+def pair_products(even, odd, left_ref, right_ref):
     block = left_ref.shape[0]
     tiles, _, width = even.shape
     upper = lax.broadcasted_iota(jnp.int32, even.shape, 1) < 4
@@ -105,7 +119,6 @@
     left = left_ref[...]
     inner = dot(left, source).astype(BF16)
     flipped = lax.dot_general(left, target, CONTRACT_ROWS, preferred_element_type=F32).astype(BF16)
-    right_copy.wait()
     right = right_ref[...]
     forward = dot(inner, right).reshape(tiles, 8, width)
     adjoint = lax.dot_general(
@@ -118,17 +131,15 @@
 
 
 def first_pair_kernel(
-    fetched_ref, left_ref, right_hbm, wave_ref, diag_ref, out_ref, right_ref, done
+    fetched_ref, left_ref, right_ref, wave_ref, diag_ref, near_ref, out_ref
 ):
-    copy = pltpu.make_async_copy(right_hbm, right_ref, done)
-    copy.start()
     width = right_ref.shape[0]
     tiles = left_ref.shape[0] // 8
     blocks, _, groups, slots, _, share = out_ref.shape
     far = slots - 1
     fetched = fetched_ref[...].astype(F32).reshape(tiles, 2, 8, width)
     even, odd = fetched[:, 0], fetched[:, 1]
-    products = pair_products(even, odd, left_ref, right_ref, copy)
+    products = pair_products(even, odd, left_ref, right_ref)
     for block in range(blocks):
         for parity, product in enumerate(products):
             for grp in range(groups):
@@ -152,9 +163,7 @@
                 out_ref[block, parity, grp, far] = carried
 
 
-def second_pair_kernel(fetched_ref, left_ref, right_hbm, out_ref, right_ref, done):
-    copy = pltpu.make_async_copy(right_hbm, right_ref, done)
-    copy.start()
+def second_pair_kernel(fetched_ref, left_ref, right_ref, out_ref):
     groups, share = fetched_ref.shape[2], fetched_ref.shape[4]
     even, odd = (
         jnp.concatenate(
@@ -162,7 +171,7 @@
         )
         for parity in range(2)
     )
-    products = pair_products(even, odd, left_ref, right_ref, copy)
+    products = pair_products(even, odd, left_ref, right_ref)
     for parity, product in enumerate(products):
         for grp in range(groups):
             out_ref[:, parity, grp] = product[:, :, grp * share : (grp + 1) * share].astype(BF16)
@@ -209,19 +218,15 @@
     out_ref[...] = base_ref[...] + dot(every_ref[...], arrived_ref[...])
 
 
-def call(kernel, outs, flops, *args, scratch=(), far_away=()):
+def call(kernel, outs, flops, *args, grant=24):
     specs = jax.tree.map(lambda _: VMEM, outs)
     size = sum(arg.size * arg.dtype.itemsize for arg in args)
     return pl.pallas_call(
         kernel,
         out_shape=outs,
-        in_specs=[
-            pl.BlockSpec(memory_space=pltpu.HBM) if at in far_away else VMEM
-            for at in range(len(args))
-        ],
+        in_specs=[VMEM] * len(args),
         out_specs=specs,
-        scratch_shapes=scratch,
-        compiler_params=pltpu.CompilerParams(vmem_limit_bytes=24 << 20),
+        compiler_params=pltpu.CompilerParams(vmem_limit_bytes=grant << 20),
         cost_estimate=pl.CostEstimate(flops=flops, bytes_accessed=2 * size, transcendentals=0),
     )(*args)
 
@@ -245,21 +250,28 @@
     share = width // groups
     messages = 2 * ops * rows_here
     left, right = left_ops[0], right_ops[0]
-    wave = wave.reshape(rows, width)
-    diag = diag_energy.reshape(rows, width)
-    held = (pltpu.VMEM(right.shape, BF16), pltpu.SemaphoreType.DMA)
-    near_choose, every, outgoing = call(
-        functools.partial(select_kernel, groups, near // blocks),
+    pairs, slots = pair_sectors.T, sector_slot[None]
+    outgoing = call(
+        functools.partial(select_kernel, groups),
+        array((messages, width), BF16),
+        200_000_000,
+        pairs,
+        slots,
+        wave,
+        grant=60,
+    )
+    near_choose, every = call(
+        functools.partial(table_kernel, groups, near // blocks),
         (
             array((rows, 2 * near * rows_here), BF16),
             array((rows, groups * messages), BF16),
-            array((messages, width), BF16),
         ),
-        400_000_000,
-        pair_sectors.T,
-        sector_slot[None],
-        wave,
-    )
+        2_000_000_000,
+        pairs,
+        slots,
+    )
+    wave = wave.reshape(rows, width)
+    diag = diag_energy.reshape(rows, width)
     fetched = exchange(outgoing.reshape(ops, -1, width), OPS).reshape(messages, width)
     scattered = call(
         first_pair_kernel,
@@ -270,8 +282,7 @@
         right,
         wave,
         diag,
-        scratch=held,
-        far_away=(2,),
+        near_choose,
     )
     arrived = exchange(scattered.reshape(near, far + 1, 8, share), NEAR)
     partial = call(
@@ -300,8 +311,6 @@
         fetched.reshape(shape),
         left,
         right,
-        scratch=held,
-        far_away=(2,),
     )
     arrived = exchange(scattered.reshape(ops * groups, -1, share), OPS_GRP)
     sigma_out = call(

time: 201 us -> 198 us (0.985)
  local copies, waits for them, and re-layouts: 3.42 us -> 1.2 us
    pallas_call x6 -> x7, Pallas kernels: 7.94 us -> 8.86 us  [call(): pl.pallas_call(kernel, out_shape=outs, in_specs=[VMEM] * len(args), out_s...]
where the time goes in v4:
time: 198 us
  blocking collectives  136 us (69%)
  waiting for transfers between devices  30.3 us (15%)
  starting transfers between devices  20.9 us (11%)
  Pallas kernels  8.86 us (4%)
    all_to_all x4, blocking collectives, exchange(): return lax.all_to_all(value, axes, 0, 0, tiled=True)  136 us
    all_to_all x1, waiting for transfers between devices, exchange(): return lax.all_to_all(value, axes, 0, 0, tiled=True)  30.3 us
    all_to_all x1, starting transfers between devices, exchange(): return lax.all_to_all(value, axes, 0, 0, tiled=True)  20.9 us
    pallas_call x7, Pallas kernels, call(): pl.pallas_call(kernel, out_shape=outs, in_specs=[VMEM] * len(args), out_s...  8.86 us
  transfers between devices with their start and end apart: 1, of which 1 were waited for; matrix products, arithmetic and copies ran while one was open for 0% of the time, Pallas kernels for 0%

profile of v4, /device:TPU:1, one launch (start us, length us, event | category | flops | bytes accessed | tf_op | source)
XLA Modules:
  0.0 198.1 jit_solution(12219956209495978803)
XLA Ops:
  0.6 2.8 %shard_map.78 = bf16[1024,512]{1,0:T(8,128)(2,1)} custom-call(s32[2,512]{1,0:T(2,128)} %bitcast.19, s32[1,32]{1,0:T(1,128)} %bitcast.21, bf16[32,4,512]{2,1,0:T(4,128)(2,1)} %wave_ref.1), custom_call_target="tpu_custom_call" | custom-call | flops 200000000 | bytes 270592 | tf_op jit(solution)/shard_map/pallas_call | solution.py:224
  3.4 0.0 copy-start.5
  3.4 0.0 copy-start.6
  3.4 0.0 copy-start
  3.4 0.0 copy-start.1
  3.4 20.9 %all-to-all-start = ((bf16[128,8,512]{2,1,0:T(8,128)(2,1)}), bf16[128,8,512]{2,1,0:T(8,128)(2,1)S(1)}, u32[]{:S(2)}, u32[]{:S(2)}) async-start(bf16[128,8,512]{2,1,0:T(8,128)(2,1)} %bitcast.27), calls=%async_computation | async-start | bytes 2097152 | tf_op jit(solution)/shard_map/all_to_all | solution.py:239
  24.4 0.0 copy-done.5
  24.4 0.0 copy-done.6
  24.4 0.1 reshape.40.diag_ref
  24.5 0.0 copy-done
  24.5 0.0 copy-done.1
  24.6 0.0 copy-start.2
  24.6 0.7 shard_map.77
  25.3 30.3 %all-to-all-done = bf16[128,8,512]{2,1,0:T(8,128)(2,1)S(1)} async-done(((bf16[128,8,512]{2,1,0:T(8,128)(2,1)}), bf16[128,8,512]{2,1,0:T(8,128)(2,1)S(1)}, u32[]{:S(2)}, u32[]{:S(2)}) %all-to-all-start) | async-done | bytes 1048608 | tf_op jit(solution)/shard_map/all_to_all | solution.py:239
  55.6 0.0 copy-done.2
  55.6 0.0 copy-start.3
  55.6 1.0 copy-done.3
  56.6 1.6 shard_map.79
  58.3 23.1 %all_to_all.25.arrived_ref = bf16[32,17,8,128]{3,2,1,0:T(8,128)(2,1)S(1)} all-to-all(bf16[32,17,8,128]{3,2,1,0:T(8,128)(2,1)S(1)} %bitcast.14), channel_id=1, replica_groups=mesh['ops_0'=4,'ops_1'=4,'ops_2'=4,'ops_3'=2,'grp'=4] {'ops_0','ops_3','..., dimensions={0} | all-to-all | bytes 2228224 | tf_op jit(solution)/shard_map/all_to_all | solution.py:239
  81.4 0.4 shard_map.80
  81.8 24.7 %all_to_all.26.arrived_ref = bf16[16,136,128]{2,1,0:T(8,128)(2,1)S(1)} all-to-all(bf16[16,136,128]{2,1,0:T(8,128)(2,1)S(1)} %shard_map.80), channel_id=1, replica_groups=mesh['ops_0'=4,'ops_1'=4,'ops_2'=4,'ops_3'=2,'grp'=4] {'ops_1','ops_2'}, dimensions={0} | all-to-all | bytes 1114112 | tf_op jit(solution)/shard_map/all_to_all | solution.py:239
  106.5 0.8 shard_map.81
  107.3 0.0 copy-start.4
  107.3 44.6 %all_to_all.27 = bf16[512,8,128]{2,1,0:T(8,128)(2,1)S(1)} all-to-all(bf16[512,8,128]{2,1,0:T(8,128)(2,1)S(1)} %bitcast.16), channel_id=1, replica_groups=mesh['ops_0'=4,'ops_1'=4,'ops_2'=4,'ops_3'=2,'grp'=4] {'ops_0','ops_1','..., dimensions={0} | all-to-all | bytes 2097152 | tf_op jit(solution)/shard_map/all_to_all | solution.py:239
  151.9 0.0 copy-done.4
  151.9 1.5 shard_map.82
  153.4 43.6 %all_to_all.28 = bf16[512,8,128]{2,1,0:T(8,128)(2,1)S(1)} all-to-all(bf16[512,8,128]{2,1,0:T(8,128)(2,1)S(1)} %bitcast.18), channel_id=1, replica_groups=mesh['ops_0'=4,'ops_1'=4,'ops_2'=4,'ops_3'=2,'grp'=4] {'ops_0','ops_1','..., dimensions={0} | all-to-all | bytes 2097152 | tf_op jit(solution)/shard_map/all_to_all | solution.py:239
  197.0 1.1 shard_map.83
  (1 shorter events, 0.0 us)
Async XLA Ops:
  3.4 21.0 %copy-start.5 = (bf16[32,4,512]{2,1,0:T(4,128)(2,1)S(1)}, bf16[32,4,512]{2,1,0:T(4,128)(2,1)}, u32[]{:S(2)}) copy-start(bf16[32,4,512]{2,1,0:T(4,128)(2,1)} %wave_ref.1) | copy-start | bytes 393220
  3.4 21.0 %copy-start.6 = (f32[32,4,512]{2,1,0:T(4,128)S(1)}, f32[32,4,512]{2,1,0:T(4,128)}, u32[]{:S(2)}) copy-start(f32[32,4,512]{2,1,0:T(4,128)} %param.7) | copy-start | bytes 786436
  3.4 21.1 %copy-start = (s32[512,2]{0,1:T(2,128)S(1)}, s32[512,2]{0,1:T(2,128)}, u32[]{:S(2)}) copy-start(s32[512,2]{0,1:T(2,128)} %param.10) | copy-start | bytes 12292
  3.4 21.1 %copy-start.1 = (s32[32]{0:T(128)S(1)}, s32[32]{0:T(128)}, u32[]{:S(2)}) copy-start(s32[32]{0:T(128)} %param.11) | copy-start | bytes 388
  3.4 52.2 %all-to-all-start = ((bf16[128,8,512]{2,1,0:T(8,128)(2,1)}), bf16[128,8,512]{2,1,0:T(8,128)(2,1)S(1)}, u32[]{:S(2)}, u32[]{:S(2)}) async-start(bf16[128,8,512]{2,1,0:T(8,128)(2,1)} %bitcast.27), calls=%async_computation | async-start | bytes 2097152 | tf_op jit(solution)/shard_map/all_to_all | solution.py:239
  24.6 31.0 %copy-start.2 = (bf16[1,512,512]{2,1,0:T(8,128)(2,1)S(1)}, bf16[1,512,512]{2,1,0:T(8,128)(2,1)}, u32[]{:S(2)}) copy-start(bf16[1,512,512]{2,1,0:T(8,128)(2,1)} %param.8) | copy-start | bytes 1572868
  55.6 1.0 copy-start.3
  107.3 44.6 %copy-start.4 = (bf16[1,512,512]{2,1,0:T(8,128)(2,1)S(1)}, bf16[1,512,512]{2,1,0:T(8,128)(2,1)}, u32[]{:S(2)}) copy-start(bf16[1,512,512]{2,1,0:T(8,128)(2,1)} %param.9) | copy-start | bytes 1572868

commit v5 on v4

--- a/solution.py
+++ b/solution.py
@@ -131,7 +131,7 @@
 
 
 def first_pair_kernel(
-    fetched_ref, left_ref, right_ref, wave_ref, diag_ref, near_ref, out_ref
+    fetched_ref, left_ref, right_ref, wave_ref, diag_ref, out_ref
 ):
     width = right_ref.shape[0]
     tiles = left_ref.shape[0] // 8
@@ -269,9 +269,12 @@
         2_000_000_000,
         pairs,
         slots,
+        grant=60,
     )
     wave = wave.reshape(rows, width)
-    diag = diag_energy.reshape(rows, width)
+    diag, near_choose, every = lax.optimization_barrier(
+        (diag_energy.reshape(rows, width), near_choose, every)
+    )
     fetched = exchange(outgoing.reshape(ops, -1, width), OPS).reshape(messages, width)
     scattered = call(
         first_pair_kernel,
@@ -282,7 +285,6 @@
         right,
         wave,
         diag,
-        near_choose,
     )
     arrived = exchange(scattered.reshape(near, far + 1, 8, share), NEAR)
     partial = call(

time: 198 us -> 197 us (level)
  transfers between devices with their start and end apart: 1 -> 1, of which waited for: 1 -> 1; matrix products, arithmetic and copies ran while one was open for 0% -> 0% of each run, Pallas kernels for 0% -> 1%
where the time goes in v5:
time: 197 us
  blocking collectives  136 us (69%)
  waiting for transfers between devices  28.7 us (15%)
  starting transfers between devices  20.9 us (11%)
  Pallas kernels  10.5 us (5%)
    all_to_all x4, blocking collectives, exchange(): return lax.all_to_all(value, axes, 0, 0, tiled=True)  136 us
    all_to_all x1, waiting for transfers between devices, exchange(): return lax.all_to_all(value, axes, 0, 0, tiled=True)  28.7 us
    all_to_all x1, starting transfers between devices, exchange(): return lax.all_to_all(value, axes, 0, 0, tiled=True)  20.9 us
    pallas_call x7, Pallas kernels, call(): pl.pallas_call(kernel, out_shape=outs, in_specs=[VMEM] * len(args), out_s...  10.5 us
  transfers between devices with their start and end apart: 1, of which 1 were waited for; matrix products, arithmetic and copies ran while one was open for 0% of the time, Pallas kernels for 1%

profile of v5, /device:TPU:1, one launch (start us, length us, event | category | flops | bytes accessed | tf_op | source)
XLA Modules:
  0.0 197.1 jit_solution(2880186841889021910)
XLA Ops:
  0.6 2.8 %shard_map.78 = bf16[1024,512]{1,0:T(8,128)(2,1)} custom-call(s32[2,512]{1,0:T(2,128)} %bitcast.25, s32[1,32]{1,0:T(1,128)} %bitcast.27, bf16[32,4,512]{2,1,0:T(4,128)(2,1)} %wave_ref.1), custom_call_target="tpu_custom_call" | custom-call | flops 200000000 | bytes 270592 | tf_op jit(solution)/shard_map/pallas_call | solution.py:224
  3.5 0.0 copy-start.4
  3.5 0.0 copy-start.5
  3.5 20.9 %all-to-all-start = ((bf16[128,8,512]{2,1,0:T(8,128)(2,1)}), bf16[128,8,512]{2,1,0:T(8,128)(2,1)S(1)}, u32[]{:S(2)}, u32[]{:S(2)}) async-start(bf16[128,8,512]{2,1,0:T(8,128)(2,1)} %bitcast.23), calls=%async_computation | async-start | bytes 2097152 | tf_op jit(solution)/shard_map/all_to_all | solution.py:239
  24.4 0.0 copy-done.4
  24.4 0.0 copy-done.5
  24.5 0.1 reshape.37.diag_ref
  24.6 0.0 copy-start.2
  24.6 0.0 copy-start.3
  24.6 2.3 %shard_map.77 = (bf16[128,256]{1,0:T(8,128)(2,1)}, bf16[128,4096]{1,0:T(8,128)(2,1)}) custom-call(s32[2,512]{1,0:T(2,128)} %bitcast.26, s32[1,32]{1,0:T(1,128)} %bitcast.28), custom_call_target="tpu_custom_call" | custom-call | flops 2000000000 | bytes 8448 | tf_op jit(solution)/shard_map/pallas_call | solution.py:224
  26.9 28.7 %all-to-all-done = bf16[128,8,512]{2,1,0:T(8,128)(2,1)S(1)} async-done(((bf16[128,8,512]{2,1,0:T(8,128)(2,1)}), bf16[128,8,512]{2,1,0:T(8,128)(2,1)S(1)}, u32[]{:S(2)}, u32[]{:S(2)}) %all-to-all-start) | async-done | bytes 1048608 | tf_op jit(solution)/shard_map/all_to_all | solution.py:239
  55.6 0.0 copy-done.2
  55.6 0.0 copy-done.3
  55.6 1.6 shard_map.79
  57.2 0.0 copy-start.1
  57.3 23.3 %all_to_all.25.arrived_ref = bf16[32,17,8,128]{3,2,1,0:T(8,128)(2,1)S(1)} all-to-all(bf16[32,17,8,128]{3,2,1,0:T(8,128)(2,1)S(1)} %bitcast.14), channel_id=1, replica_groups=mesh['ops_0'=4,'ops_1'=4,'ops_2'=4,'ops_3'=2,'grp'=4] {'ops_0','ops_3','..., dimensions={0} | all-to-all | bytes 2228224 | tf_op jit(solution)/shard_map/all_to_all | solution.py:239
  80.5 0.0 copy-done.1
  80.5 0.0 copy-start
  80.5 0.4 shard_map.80
  81.0 24.7 %all_to_all.26.arrived_ref = bf16[16,136,128]{2,1,0:T(8,128)(2,1)S(1)} all-to-all(bf16[16,136,128]{2,1,0:T(8,128)(2,1)S(1)} %shard_map.80), channel_id=1, replica_groups=mesh['ops_0'=4,'ops_1'=4,'ops_2'=4,'ops_3'=2,'grp'=4] {'ops_1','ops_2'}, dimensions={0} | all-to-all | bytes 1114112 | tf_op jit(solution)/shard_map/all_to_all | solution.py:239
  105.6 0.0 copy-done
  105.6 0.8 shard_map.81
  106.4 44.5 %all_to_all.27 = bf16[512,8,128]{2,1,0:T(8,128)(2,1)S(1)} all-to-all(bf16[512,8,128]{2,1,0:T(8,128)(2,1)S(1)} %bitcast.16), channel_id=1, replica_groups=mesh['ops_0'=4,'ops_1'=4,'ops_2'=4,'ops_3'=2,'grp'=4] {'ops_0','ops_1','..., dimensions={0} | all-to-all | bytes 2097152 | tf_op jit(solution)/shard_map/all_to_all | solution.py:239
  150.9 1.5 shard_map.82
  152.4 43.6 %all_to_all.28 = bf16[512,8,128]{2,1,0:T(8,128)(2,1)S(1)} all-to-all(bf16[512,8,128]{2,1,0:T(8,128)(2,1)S(1)} %bitcast.18), channel_id=1, replica_groups=mesh['ops_0'=4,'ops_1'=4,'ops_2'=4,'ops_3'=2,'grp'=4] {'ops_0','ops_1','..., dimensions={0} | all-to-all | bytes 2097152 | tf_op jit(solution)/shard_map/all_to_all | solution.py:239
  196.0 1.1 shard_map.83
  (1 shorter events, 0.0 us)
Async XLA Ops:
  3.5 20.9 %copy-start.4 = (bf16[32,4,512]{2,1,0:T(4,128)(2,1)S(1)}, bf16[32,4,512]{2,1,0:T(4,128)(2,1)}, u32[]{:S(2)}) copy-start(bf16[32,4,512]{2,1,0:T(4,128)(2,1)} %wave_ref.1) | copy-start | bytes 393220
  3.5 21.0 %copy-start.5 = (f32[32,4,512]{2,1,0:T(4,128)S(1)}, f32[32,4,512]{2,1,0:T(4,128)}, u32[]{:S(2)}) copy-start(f32[32,4,512]{2,1,0:T(4,128)} %param.7) | copy-start | bytes 786436
  3.5 52.1 %all-to-all-start = ((bf16[128,8,512]{2,1,0:T(8,128)(2,1)}), bf16[128,8,512]{2,1,0:T(8,128)(2,1)S(1)}, u32[]{:S(2)}, u32[]{:S(2)}) async-start(bf16[128,8,512]{2,1,0:T(8,128)(2,1)} %bitcast.23), calls=%async_computation | async-start | bytes 2097152 | tf_op jit(solution)/shard_map/all_to_all | solution.py:239
  24.6 31.0 %copy-start.2 = (bf16[1,512,512]{2,1,0:T(8,128)(2,1)S(1)}, bf16[1,512,512]{2,1,0:T(8,128)(2,1)}, u32[]{:S(2)}) copy-start(bf16[1,512,512]{2,1,0:T(8,128)(2,1)} %param.8) | copy-start | bytes 1572868
  24.6 31.0 %copy-start.3 = (bf16[1,512,512]{2,1,0:T(8,128)(2,1)S(1)}, bf16[1,512,512]{2,1,0:T(8,128)(2,1)}, u32[]{:S(2)}) copy-start(bf16[1,512,512]{2,1,0:T(8,128)(2,1)} %param.9) | copy-start | bytes 1572868
  57.2 23.3 %copy-start.1 = (bf16[128,256]{1,0:T(8,128)(2,1)S(1)}, bf16[128,256]{1,0:T(8,128)(2,1)}, u32[]{:S(2)}) copy-start(bf16[128,256]{1,0:T(8,128)(2,1)} %get-tuple-element.12.near_ref) | copy-start | bytes 196612
  80.5 25.1 %copy-start = (bf16[128,4096]{1,0:T(8,128)(2,1)S(1)}, bf16[128,4096]{1,0:T(8,128)(2,1)}, u32[]{:S(2)}) copy-start(bf16[128,4096]{1,0:T(8,128)(2,1)} %get-tuple-element.14.every_ref) | copy-start | bytes 3145732
